TPU v7x, 128 devices: a whole 4x4x4 slice. The times are simulated.
128 devices in a mesh: kv: 64 (over z, x, y), head: 2 (over core).
Axes of the slice: x: 4, y: 4, z: 4, core: 2. Of those that a mesh axis runs over, the one named last changes fastest.
Arguments:
- queries: bfloat16 [8, 256, 128], P('head', 'kv'), may hold values from -384 to 384
- key_cache: bfloat16 [4096, 8, 128, 128], P('kv', 'head'), may hold values from -6 to 6
- value_cache: bfloat16 [4096, 8, 128, 128], P('kv', 'head'), may hold values from -6 to 6
- key_new: bfloat16 [32, 8, 128], P(None, 'head'), may hold values from -6 to 6
- value_new: bfloat16 [32, 8, 128], P(None, 'head'), may hold values from -6 to 6
- lengths: int32 [32], replicated, may hold values from 2 to 16385, as said below
- page_table: int32 [4096], replicated, may hold values from 0 to 4095, each once
Outputs:
- attended: bfloat16 [8, 256, 128], P('head', 'kv')
Inputs may be any that keep to these rules, and one draw needn't show every extreme that they name: The cache holds the first lengths[s] - 1 tokens of sequence s; some sequence has the largest length. `page_table`: every page appears once; page g lies on kv index g // 64.
All inputs are finite; a program needn't handle non-finite values.
Results may differ from a plain program's by a relative error of at most 0.0025.
Values may be sent and summed in bfloat16 or wider, within the bound.
No kernel may reach another device: no remote copies, remote signals or barrier semaphores. Data moves between devices by JAX's collectives and lax.ppermute only.
A program may use at most 64 MiB of HBM per device.

v0:
```python
import math

import jax
import jax.numpy as jnp
from jax import lax
from jax.sharding import PartitionSpec as P

LOWEST_SCORE = -1e30


def in_order(pieces, dim):
    pieces = jnp.moveaxis(pieces, 0, dim)
    shape = pieces.shape
    return pieces.reshape(*shape[:dim], shape[dim] * shape[dim + 1], *shape[dim + 2 :])


def from_everyone(x, axis):
    length = lax.axis_size(axis)
    return lax.all_to_all(jnp.broadcast_to(x[None], (length, *x.shape)), axis, 0, 0, tiled=True)


def collect(x, axis, dim):
    return in_order(from_everyone(x, axis), dim)


def taken_together(x, axis):
    return from_everyone(x, axis).max(axis=0)


def split_up(x, dim, length):
    shape = x.shape
    pieces = x.reshape(*shape[:dim], length, shape[dim] // length, *shape[dim + 1 :])
    return jnp.moveaxis(pieces, dim, 0)


def summed_on_arrival(x, axis, dim):
    pieces = split_up(x, dim, lax.axis_size(axis))
    arrived = lax.all_to_all(pieces, axis, split_axis=0, concat_axis=0, tiled=True)
    return arrived.sum(axis=0)


def sent_together(arrays, axis, dim, along):
    widths = [math.prod(a.shape[along:]) for a in arrays]
    both = jnp.concatenate(
        [a.reshape(*a.shape[:along], w) for a, w in zip(arrays, widths)], axis=along
    )
    result = summed_on_arrival(both, axis, dim)
    pieces = jnp.split(result, [sum(widths[:k]) for k in range(1, len(widths))], axis=along)
    return tuple(
        (b.reshape(*result.shape[:along], *a.shape[along:]) for a, b in zip(arrays, pieces))
    )


def finish(cache_max, cache_sum, cache_out, query_wide, fresh_key, fresh_value, score_scale):
    new_score = jnp.sum(query_wide * fresh_key.astype(jnp.float32), axis=-1) * score_scale
    highest = jnp.maximum(cache_max, new_score)
    old_part = jnp.exp(cache_max - highest)
    new_part = jnp.exp(new_score - highest)
    numerator = cache_out * old_part[..., None] + new_part[..., None] * fresh_value.astype(
        jnp.float32
    )
    denominator = cache_sum * old_part + new_part
    return (numerator / denominator[..., None]).astype(jnp.bfloat16)


def on_device(queries, key_cache, value_cache, key_new, value_new, lengths, page_table):
    all_query = collect(queries, "kv", 1)
    seq_count = lengths.shape[0]
    page_total = page_table.shape[0]
    pages_here = key_cache.shape[0]
    kv_here = key_cache.shape[1]
    page_len = key_cache.shape[2]
    head_width = key_cache.shape[3]
    rows_all = all_query.shape[1]
    group_size = rows_all // seq_count
    page_slots = page_total // seq_count
    local_rows = queries.shape[1]
    score_scale = 1.0 / math.sqrt(head_width)
    kv_index = lax.axis_index("kv")
    inverse = (
        jnp.zeros((page_total,), jnp.int32)
        .at[page_table]
        .set(jnp.arange(page_total, dtype=jnp.int32))
    )
    local_ids = lax.dynamic_slice_in_dim(inverse, kv_index * pages_here, pages_here)
    page_seq = local_ids // page_slots
    page_slot = local_ids % page_slots
    grouped = all_query.reshape(kv_here, seq_count, group_size, head_width)
    page_query = grouped[:, page_seq]
    scores = (
        jnp.einsum("gpqd,pgtd->pgqt", page_query, key_cache, preferred_element_type=jnp.float32)
        * score_scale
    )
    positions = page_slot[:, None] * page_len + jnp.arange(page_len, dtype=jnp.int32)[None, :]
    in_cache = (positions < (lengths[page_seq] - 1)[:, None])[:, None, None, :]
    masked = jnp.where(in_cache, scores, LOWEST_SCORE)
    page_max = jnp.max(masked, axis=3)
    weights = jnp.where(in_cache, jnp.exp(masked - page_max[..., None]), 0.0)
    page_sum = jnp.sum(weights, axis=3)
    page_out = jnp.einsum(
        "pgqt,pgtd->pgqd",
        weights.astype(jnp.bfloat16),
        value_cache,
        preferred_element_type=jnp.float32,
    )
    member = page_seq[None, :] == jnp.arange(seq_count, dtype=jnp.int32)[:, None]
    seq_best = jnp.max(jnp.where(member[:, :, None, None], page_max[None], LOWEST_SCORE), axis=1)
    factor = jnp.exp(page_max - seq_best[page_seq])
    onehot = member.astype(jnp.float32)
    seq_sum = jnp.einsum("sp,pgq->gsq", onehot, page_sum * factor, precision=lax.Precision.HIGHEST)
    seq_out = jnp.einsum(
        "sp,pgqd->gsqd", onehot, page_out * factor[..., None], precision=lax.Precision.HIGHEST
    )
    seq_max = jnp.transpose(seq_best, (1, 0, 2)).reshape(kv_here, rows_all)
    seq_sum = seq_sum.reshape(kv_here, rows_all)
    seq_out = seq_out.reshape(kv_here, rows_all, head_width)
    global_max = taken_together(seq_max, "kv")
    rescale = jnp.exp(seq_max - global_max)
    cache_out, cache_sum = sent_together(
        (seq_out * rescale[..., None], seq_sum * rescale), "kv", 1, 2
    )
    cache_max = lax.dynamic_slice_in_dim(global_max, kv_index * local_rows, local_rows, 1)
    row_seq = (kv_index * local_rows + jnp.arange(local_rows, dtype=jnp.int32)) // group_size
    fresh_key = jnp.transpose(key_new[row_seq], (1, 0, 2))
    fresh_value = jnp.transpose(value_new[row_seq], (1, 0, 2))
    query_wide = queries.astype(jnp.float32)
    return finish(cache_max, cache_sum, cache_out, query_wide, fresh_key, fresh_value, score_scale)


def solution(mesh):
    placed = (
        P("head", "kv", None),
        P("kv", "head", None, None),
        P("kv", "head", None, None),
        P(None, "head", None),
        P(None, "head", None),
        P(),
        P(),
    )
    return jax.shard_map(
        on_device, mesh=mesh, in_specs=placed, out_specs=P("head", "kv", None), check_vma=False
    )
```

profile of v0, /device:TPU:0, one launch (start us, length us, event | category | flops | bytes accessed | tf_op | source)
XLA Modules:
  0.0 90.9 jit_solution(1076743474031147585)
XLA Ops:
  0.0 0.0 copy-start
  0.0 1.5 %broadcast_in_dim.78 = bf16[64,4,4,128]{3,2,1,0:T(4,128)(2,1)} broadcast(bf16[4,4,128]{2,1,0:T(4,128)(2,1)} %param.7), dimensions={1,2,3} | broadcast | bytes 266240 | tf_op jit(solution)/shard_map/broadcast_in_dim | solution.py:19
  1.5 11.5 %all-to-all-start = ((bf16[64,4,4,128]{3,2,1,0:T(4,128)(2,1)}), bf16[64,4,4,128]{3,2,1,0:T(4,128)(2,1)S(1)}, u32[]{:S(2)}, u32[]{:S(2)}) async-start(bf16[64,4,4,128]{3,2,1,0:T(4,128)(2,1)} %broadcast_in_dim.78), calls=%async_computation | async-start | bytes 524288 | tf_op jit(solution)/shard_map/all_to_all | solution.py:19
  13.0 0.7 compare_select_fusion
  13.7 15.5 %scatter_custom_fusion = s32[4096]{0:T(1024)S(1)} fusion(s32[4096]{0:T(1024)S(1)} %compare_select_fusion, s32[4096]{0:T(1024)S(1)} %iota.23, s32[]{:T(128)} %constant.32.clone.1), kind=kCustom, calls=%fused_computation.40 | custom fusion | bytes 16388 | tf_op jit(solution)/shard_map/scatter | solution.py:83
  29.3 0.1 fusion.22
  29.3 0.1 compare_select_fusion.2
  29.4 1.4 %gather_fusion = s32[64]{0:T(128)S(1)} fusion(s32[32]{0:T(128)} %param.12, s32[1024]{0:T(1024)S(1)} %pad_clamp_fusion.1), kind=kCustom, calls=%fused_computation | custom fusion | bytes 768 | tf_op jit(solution)/shard_map/gather | solution.py:95
  30.9 0.1 add_compare_fusion
  31.0 0.0 all-to-all-done
  31.0 0.1 copy.90
  31.1 0.8 gather_fusion.1
  31.9 6.9 %fusion.28 = (f32[64,4,8]{2,1,0:T(4,128)S(1)}, f32[64,4,8,128]{3,2,1,0:T(8,128)S(1)}) fusion(bf16[64,4,128,128]{3,2,1,0:T(8,128)(2,1)} %param.8, bf16[64,4,8,128]{3,2,1,0:T(8,128)(2,1)S(1)} %gather_fusion.1, pred[64,128]{1,0:T(8,128)(4,1)S(1)} %add_compare_fusion), kind=kOutput, calls=%fused_computation.66 | convolution fusion | flops 67893248 | bytes 9977856 | tf_op jit(solution)/shard_map/gpqd,pgtd->pgqt/dot_general | solution.py:91
  38.8 0.1 copy.91
  38.9 0.3 select_reduce_fusion
  39.2 0.7 gather_fusion.2
  39.9 0.8 fusion.2
  40.6 0.1 broadcast_in_dim.84
  40.7 0.7 broadcast_in_dim.85
  41.5 10.3 %all-to-all-start.1 = ((f32[64,4,256]{2,1,0:T(4,128)}), f32[64,4,256]{2,1,0:T(4,128)S(1)}, u32[]{:S(2)}, u32[]{:S(2)}) async-start(f32[64,4,256]{2,1,0:T(4,128)} %broadcast_in_dim.85), calls=%async_computation.1 | async-start | bytes 524288 | tf_op jit(solution)/shard_map/all_to_all | solution.py:19
  51.9 4.7 %convolution_multiply_fusion = f32[64,4,8,128]{3,2,1,0:T(8,128)S(1)} fusion(bf16[64,4,128,128]{3,2,1,0:T(8,128)(2,1)} %param.9, f32[64,4,8,128]{3,2,1,0:T(8,128)S(1)} %get-tuple-element.15, f32[64,4,8]{2,1,0:T(4,128)S(1)} %bitcast.50, f32[64,4,8]{2,1,0:T(4,128)S(1)} %get-tuple-element.14, pred[64,128]{1,0:T(8,128)(4,1)S(1)} %add_compare_fusion), kind=kOutput, calls=%fused_computation.6 | convolution fusion | flops 68157440 | bytes 10510336 | tf_op jit(solution)/shard_map/pgqt,pgtd->pgqd/dot_general | solution.py:100
  56.6 0.0 copy-start.1
  56.6 1.1 %convolution_bitcast_fusion = f32[4,32,8,128]{3,1,2,0:T(8,128)S(1)} fusion(f32[64,4,8,128]{3,2,1,0:T(8,128)S(1)} %convolution_multiply_fusion, s32[64]{0:T(128)S(1)} %get-tuple-element.13), kind=kOutput, calls=%fused_computation.9 | convolution fusion | flops 100665344 | bytes 1573120 | tf_op jit(solution)/shard_map/sp,pgqd->gsqd/dot_general | solution.py:111
  57.7 0.1 reshape.189
  57.8 0.1 reshape.191
  57.9 0.3 copy.93
  58.2 0.3 convolution_bitcast_fusion.1
  58.5 0.1 copy.98
  58.5 0.1 reshape.190
  58.7 0.1 copy.102
  58.7 0.1 copy.100
  58.9 3.5 %all-to-all-done.1 = f32[64,4,256]{2,1,0:T(4,128)S(1)} async-done(((f32[64,4,256]{2,1,0:T(4,128)}), f32[64,4,256]{2,1,0:T(4,128)S(1)}, u32[]{:S(2)}, u32[]{:S(2)}) %all-to-all-start.1) | async-done | bytes 262176 | tf_op jit(solution)/shard_map/all_to_all | solution.py:19
  62.4 0.1 reduce_max.33
  62.5 0.1 reduce_max.34
  62.6 0.1 reduce_max.35
  62.8 0.1 copy.101
  62.9 0.3 copy.103
  63.2 0.3 broadcast_multiply_fusion
  63.6 0.3 maximum_bitcast_fusion
  63.8 1.3 %copy.104 = f32[64,4,4,129]{3,2,1,0:T(4,128)} copy(f32[64,4,4,129]{3,2,0,1:T(4,128)S(1)} %maximum_bitcast_fusion) | data formatting | bytes 1056768 | tf_op jit(solution)/shard_map/transpose | solution.py:33
  65.1 6.8 %all-to-all-start.2 = ((f32[64,4,4,129]{3,2,1,0:T(4,128)}), f32[64,4,4,129]{3,2,1,0:T(4,128)S(1)}, u32[]{:S(2)}, u32[]{:S(2)}) async-start(f32[64,4,4,129]{3,2,1,0:T(4,128)} %copy.104), calls=%async_computation.2 | async-start | bytes 2097152 | tf_op jit(solution)/shard_map/all_to_all | solution.py:38
  72.0 0.0 copy-done
  72.0 0.6 gather_fusion.3
  72.6 0.0 copy-done.1
  72.6 0.1 fusion.14
  72.7 0.1 copy.108
  72.8 1.3 %gather_fusion.4 = bf16[4,4,128]{2,1,0:T(4,128)(2,1)S(1)} fusion(bf16[32,4,128]{2,1,0:T(4,128)(2,1)} %param.11, s32[1024]{0:T(1024)S(1)} %pad_clamp_fusion), kind=kCustom, calls=%fused_computation.4 | custom fusion | bytes 8208 | tf_op jit(solution)/shard_map/gather | solution.py:125
  74.1 15.5 %all-to-all-done.2 = f32[64,4,4,129]{3,2,1,0:T(4,128)S(1)} async-done(((f32[64,4,4,129]{3,2,1,0:T(4,128)}), f32[64,4,4,129]{3,2,1,0:T(4,128)S(1)}, u32[]{:S(2)}, u32[]{:S(2)}) %all-to-all-start.2) | async-done | bytes 528416 | tf_op jit(solution)/shard_map/all_to_all | solution.py:38
  89.6 0.2 reduce_sum.28
  89.8 0.1 slice_reduce_fusion
  89.9 0.1 multiply_add_fusion
  89.9 0.1 copy.109
  90.0 0.1 copy.110
  90.1 0.1 copy.111
  90.2 0.1 fusion.19
  90.3 0.6 copy.112
  (11 shorter events, 0.1 us)
Async XLA Ops:
  0.0 72.0 %copy-start = (bf16[32,4,128]{2,1,0:T(4,128)(2,1)S(1)}, bf16[32,4,128]{2,1,0:T(4,128)(2,1)}, u32[]{:S(2)}) copy-start(bf16[32,4,128]{2,1,0:T(4,128)(2,1)} %param.10) | copy-start | bytes 98308
  1.5 29.5 %all-to-all-start = ((bf16[64,4,4,128]{3,2,1,0:T(4,128)(2,1)}), bf16[64,4,4,128]{3,2,1,0:T(4,128)(2,1)S(1)}, u32[]{:S(2)}, u32[]{:S(2)}) async-start(bf16[64,4,4,128]{3,2,1,0:T(4,128)(2,1)} %broadcast_in_dim.78), calls=%async_computation | async-start | bytes 524288 | tf_op jit(solution)/shard_map/all_to_all | solution.py:19
  41.5 20.9 %all-to-all-start.1 = ((f32[64,4,256]{2,1,0:T(4,128)}), f32[64,4,256]{2,1,0:T(4,128)S(1)}, u32[]{:S(2)}, u32[]{:S(2)}) async-start(f32[64,4,256]{2,1,0:T(4,128)} %broadcast_in_dim.85), calls=%async_computation.1 | async-start | bytes 524288 | tf_op jit(solution)/shard_map/all_to_all | solution.py:19
  56.6 16.0 %copy-start.1 = (bf16[4,4,128]{2,1,0:T(4,128)(2,1)S(1)}, bf16[4,4,128]{2,1,0:T(4,128)(2,1)}, u32[]{:S(2)}) copy-start(bf16[4,4,128]{2,1,0:T(4,128)(2,1)} %param.7) | copy-start | bytes 12292
  65.1 24.4 %all-to-all-start.2 = ((f32[64,4,4,129]{3,2,1,0:T(4,128)}), f32[64,4,4,129]{3,2,1,0:T(4,128)S(1)}, u32[]{:S(2)}, u32[]{:S(2)}) async-start(f32[64,4,4,129]{3,2,1,0:T(4,128)} %copy.104), calls=%async_computation.2 | async-start | bytes 2097152 | tf_op jit(solution)/shard_map/all_to_all | solution.py:38
where the time goes:
time: 91.4 us; the launch traced here: 90.9 us
  starting transfers between devices  28.7 us (31%)
  local copies, waits for them, and re-layouts  26.6 us (29%)
  waiting for transfers between devices  19 us (21%)
  matrix products  13 us (14%)
  other arithmetic  3.3 us (4%)
    all_to_all x2, starting transfers between devices, from_everyone(): lax.all_to_all(jnp.broadcast_to(x[None], (length, *x.shape)), axis, 0, 0,...  21.9 us
    scatter x1, local copies, waits for them, and re-layouts, on_device(): inverse = jnp.zeros((page_total,), jnp.int32).at[page_table].set(jnp.aran...  15.5 us
    all_to_all x1, waiting for transfers between devices, summed_on_arrival(): lax.all_to_all(pieces, axis, split_axis=0, concat_axis=0, tiled=True)  15.5 us
    dot_general x1, matrix products, on_device(): jnp.einsum('gpqd,pgtd->pgqt', page_query, key_cache, preferred_element_ty...  6.95 us
    all_to_all x1, starting transfers between devices, summed_on_arrival(): lax.all_to_all(pieces, axis, split_axis=0, concat_axis=0, tiled=True)  6.82 us
    dot_general x1, matrix products, on_device(): jnp.einsum('pgqt,pgtd->pgqd', weights.astype(jnp.bfloat16), value_cache,...  4.74 us
    all_to_all x2, waiting for transfers between devices, from_everyone(): lax.all_to_all(jnp.broadcast_to(x[None], (length, *x.shape)), axis, 0, 0,...  3.53 us
    broadcast_in_dim x3, local copies, waits for them, and re-layouts, from_everyone(): jnp.broadcast_to(x[None], (length, *x.shape))  2.28 us
  transfers between devices with their start and end apart: 3, of which 2 were waited for; matrix products, arithmetic and copies ran while one was open for 30% of the time, Pallas kernels for 0%

commit v1 on v0

v1 whole, which is shorter than its diff:
```python
import math

import jax
import jax.numpy as jnp
from jax import lax
from jax.experimental import pallas as pl
from jax.experimental.pallas import tpu as pltpu
from jax.sharding import PartitionSpec as P

LOWEST = -1e30
GROUP = 8
MIB = 1024 * 1024


def attend_kernel(
    scale2, plan_ref, arrived_ref, k_hbm, v_hbm, send_ref,
    k_ref, v_ref, q_ref, score_ref, prob_ref, pmax_ref, max_ref, sum_ref, out_ref, k_sem, v_sem,
):
    pages = k_ref.shape[0]
    seqs, pairs = q_ref.shape[0], q_ref.shape[1]
    token = lax.broadcasted_iota(jnp.int32, (8, 128), 1)
    upper = lax.broadcasted_iota(jnp.int32, (8, 128), 0) < 4
    groups = plan_ref[pages]

    def page_of(i):
        return plan_ref[i] & (pages - 1)

    def seq_of(i):
        return (plan_ref[i] // pages) & (seqs - 1)

    def copy(hbm, vmem, sem, i):
        return pltpu.make_async_copy(hbm.at[page_of(i)], vmem.at[i], sem.at[i])

    def start(hbm, vmem, sem):
        def some(g, _):
            for u in range(GROUP):
                copy(hbm, vmem, sem, g * GROUP + u).start()
            return 0

        lax.fori_loop(0, groups, some, 0)

    start(k_hbm, k_ref, k_sem)
    start(v_hbm, v_ref, v_sem)

    max_ref[...] = jnp.full(max_ref.shape, LOWEST, jnp.float32)
    sum_ref[...] = jnp.zeros(sum_ref.shape, jnp.float32)
    out_ref[...] = jnp.zeros(out_ref.shape, jnp.float32)

    def regroup(s, _):
        for h in range(2):
            for j in range(pairs):
                q_ref[s, j, 8 * h : 8 * h + 8] = arrived_ref[2 * s + h, 8 * j : 8 * j + 8]
        return 0

    lax.fori_loop(0, seqs, regroup, 0, unroll=4)

    def each(g, body):
        for u in range(GROUP):
            body(g * GROUP + u)

    def wait_for(hbm, vmem, sem, g):
        each(g, lambda i: copy(hbm, vmem, sem, i).wait())

    def score(i):
        s = seq_of(i)
        for j in range(pairs):
            keys = k_ref[i, 2 * j : 2 * j + 2].reshape(256, 128)
            both = lax.dot_general(
                q_ref[s, j], keys, (((1,), (1,)), ((), ())), preferred_element_type=jnp.float32
            )
            for h in range(2):
                rows = slice(8 * h, 8 * h + 8)
                score_ref[i, j, h] = jnp.where(upper, both[rows, :128], both[rows, 128:])

    def weigh(i):
        s = seq_of(i)
        inside = token < plan_ref[i] // (pages * seqs)
        for j in range(pairs):
            for h in range(2):
                score = jnp.where(inside, score_ref[i, j, h], LOWEST)
                top = jnp.max(score, axis=1, keepdims=True)
                prob_ref[i, j, h] = jnp.where(inside, jnp.exp2((score - top) * scale2), 0.0)
                top = jnp.broadcast_to(top, (8, 128))
                pmax_ref[i, j, h] = top
                max_ref[s, j, h] = jnp.maximum(max_ref[s, j, h], top)

    def combine(i):
        for j in range(pairs):
            probs = jnp.concatenate([prob_ref[i, j, 0], prob_ref[i, j, 1]], axis=0)
            values = jnp.concatenate([v_ref[i, 2 * j], v_ref[i, 2 * j + 1]], axis=1)
            both = jnp.dot(probs.astype(jnp.bfloat16), values, preferred_element_type=jnp.float32)
            for h in range(2):
                rows = slice(8 * h, 8 * h + 8)
                score_ref[i, j, h] = jnp.where(upper, both[rows, :128], both[rows, 128:])

    def gather(i):
        s = seq_of(i)
        for j in range(pairs):
            for h in range(2):
                factor = jnp.exp2((pmax_ref[i, j, h] - max_ref[s, j, h]) * scale2)
                sum_ref[s, j, h] = sum_ref[s, j, h] + factor * prob_ref[i, j, h]
                out_ref[s, j, h] = out_ref[s, j, h] + factor * score_ref[i, j, h]

    def staged(hbm, vmem, sem, first, second):
        wait_for(hbm, vmem, sem, 0)
        each(0, first)

        def step(g, _):
            wait_for(hbm, vmem, sem, g)
            each(g - 1, second)
            each(g, first)
            return 0

        lax.fori_loop(1, groups, step, 0)
        each(groups - 1, second)

    staged(k_hbm, k_ref, k_sem, score, weigh)
    staged(v_hbm, v_ref, v_sem, combine, gather)

    def pack(s, _):
        for h in range(2):
            note = jnp.zeros((8, 128), jnp.float32)
            for j in range(pairs):
                send_ref[2 * s + h, 8 * j : 8 * j + 8] = out_ref[s, j, h]
                total = jnp.sum(sum_ref[s, j, h], axis=1, keepdims=True)
                note = jnp.where(token == j, max_ref[s, j, h], note)
                note = jnp.where(token == pairs + j, total, note)
            send_ref[2 * s + h, 8 * pairs :] = note
        return 0

    lax.fori_loop(0, seqs, pack, 0, unroll=4)


def merge_kernel(scale2, seq_ref, recv_ref, q_ref, k_ref, v_ref, o_ref):
    sources = recv_ref.shape[0]
    pairs = q_ref.shape[0] // 8
    lane = lax.broadcasted_iota(jnp.int32, (8, 128), 1)
    upper = lax.broadcasted_iota(jnp.int32, (8, 128), 0) < 4
    s = seq_ref[0]
    keys = k_ref[s].astype(jnp.float32)
    fresh = v_ref[s].astype(jnp.float32)
    query = q_ref[...].astype(jnp.float32)

    def spread(x, j):
        low = jnp.broadcast_to(x[2 * j : 2 * j + 1], (8, 128))
        high = jnp.broadcast_to(x[2 * j + 1 : 2 * j + 2], (8, 128))
        return jnp.where(upper, low, high)

    new = jnp.full((8, 128), LOWEST, jnp.float32)
    for j in range(pairs):
        score = jnp.sum(query[8 * j : 8 * j + 8] * spread(keys, j), axis=1, keepdims=True)
        new = jnp.where(lane == j, score, new)
    top = new
    for d in range(sources):
        top = jnp.maximum(top, recv_ref[d, 8 * pairs :])
    top = jnp.where(lane < pairs, top, 0.0)
    fresh_weight = jnp.where(lane < pairs, jnp.exp2((new - top) * scale2), 0.0)
    totals = [jnp.zeros((8, 128), jnp.float32) for _ in range(pairs)]
    outs = []
    weights = [jnp.broadcast_to(fresh_weight[:, j : j + 1], (8, 128)) for j in range(pairs)]
    for j in range(pairs):
        outs.append(weights[j] * spread(fresh, j))
    for d in range(sources):
        note = recv_ref[d, 8 * pairs :]
        weight = jnp.exp2(jnp.where(lane < pairs, note - top, 0.0) * scale2)
        for j in range(pairs):
            w = jnp.broadcast_to(weight[:, j : j + 1], (8, 128))
            totals[j] = totals[j] + w * note
            outs[j] = outs[j] + w * recv_ref[d, 8 * j : 8 * j + 8]
    for j in range(pairs):
        at = pairs + j
        total = totals[j][:, at : at + 1] + weights[j][:, at : at + 1]
        done = (outs[j] / total).astype(o_ref.dtype)
        o_ref[2 * j] = done[:4]
        o_ref[2 * j + 1] = done[4:]


def plan_pages(kv_index, pages, page_len, lengths, page_table):
    seqs = lengths.shape[0]
    total = page_table.shape[0]
    slots = total // seqs
    here = jnp.arange(pages, dtype=jnp.int32)
    hit = page_table[None, :] == (kv_index * pages + here)[:, None]
    place = jnp.sum(jnp.where(hit, jnp.arange(total, dtype=jnp.int32)[None, :], 0), axis=1)
    seq, slot = place // slots, place % slots
    owner = seq[:, None] == jnp.arange(seqs, dtype=jnp.int32)[None, :]
    length = jnp.sum(jnp.where(owner, lengths[None, :], 0), axis=1)
    inside = jnp.clip(length - 1 - slot * page_len, 0, page_len)
    used = inside > 0
    code = here + pages * (seq + seqs * inside)
    rank = jnp.sum(jnp.where(used[None, :] & (here[None, :] < here[:, None]), 1, 0), axis=1)
    put = used[None, :] & (rank[None, :] == here[:, None])
    order = jnp.sum(jnp.where(put, code[None, :], 0), axis=1)
    count = jnp.sum(jnp.where(used, 1, 0))
    groups = jnp.maximum((count + GROUP - 1) // GROUP, 1)
    return jnp.concatenate([order, jnp.broadcast_to(groups, (pages,))])


def on_device(queries, key_cache, value_cache, key_new, value_new, lengths, page_table):
    kv_here, local_rows, head_width = queries.shape
    pages_here = key_cache.shape[0]
    page_len = key_cache.shape[2]
    seq_count = lengths.shape[0]
    devices = lax.axis_size("kv")
    pairs = kv_here // 2
    rows = kv_here * local_rows
    scale2 = math.log2(math.e) / math.sqrt(head_width)
    kv_index = lax.axis_index("kv")

    mine = queries.reshape(rows, head_width)
    arrived = lax.all_to_all(
        jnp.broadcast_to(mine[None], (devices, rows, head_width)), "kv", 0, 0, tiled=True
    )
    plan = plan_pages(kv_index, pages_here, page_len, lengths, page_table)

    vmem = pl.BlockSpec(memory_space=pltpu.VMEM)
    smem = pl.BlockSpec(memory_space=pltpu.SMEM)
    hbm = pl.BlockSpec(memory_space=pltpu.HBM)
    by_page = pltpu.VMEM((pages_here, pairs, 2, 8, 128), jnp.float32)
    by_seq = pltpu.VMEM((seq_count, pairs, 2, 8, 128), jnp.float32)
    cached = pltpu.VMEM(key_cache.shape, jnp.bfloat16)
    sent = pl.pallas_call(
        lambda *refs: attend_kernel(scale2, *refs),
        out_shape=jax.ShapeDtypeStruct((devices, rows + 8, head_width), jnp.float32),
        in_specs=[smem, vmem, hbm, hbm],
        out_specs=vmem,
        scratch_shapes=[
            cached,
            cached,
            pltpu.VMEM((seq_count, pairs, 16, head_width), jnp.bfloat16),
            by_page,
            by_page,
            by_page,
            by_seq,
            by_seq,
            by_seq,
            pltpu.SemaphoreType.DMA((pages_here,)),
            pltpu.SemaphoreType.DMA((pages_here,)),
        ],
        name="attend",
        compiler_params=pltpu.CompilerParams(vmem_limit_bytes=52 * MIB),
    )(plan, arrived, key_cache, value_cache)

    received = lax.all_to_all(sent, "kv", 0, 0, tiled=True)

    return pl.pallas_call(
        lambda *refs: merge_kernel(scale2, *refs),
        out_shape=jax.ShapeDtypeStruct(queries.shape, jnp.bfloat16),
        in_specs=[smem, vmem, vmem, vmem, vmem],
        out_specs=vmem,
        name="merge",
        compiler_params=pltpu.CompilerParams(vmem_limit_bytes=8 * MIB),
    )((kv_index // 2).reshape(1).astype(jnp.int32), received, mine, key_new, value_new)


def solution(mesh):
    placed = (
        P("head", "kv", None),
        P("kv", "head", None, None),
        P("kv", "head", None, None),
        P(None, "head", None),
        P(None, "head", None),
        P(),
        P(),
    )
    return jax.shard_map(
        on_device, mesh=mesh, in_specs=placed, out_specs=P("head", "kv", None), check_vma=False
    )
```

time: 91.4 us -> 53.9 us (0.59)
  local copies, waits for them, and re-layouts: 26.6 us -> 1.44 us
  matrix products: 13 us -> 0 us
  starting transfers between devices: 28.7 us -> 17.5 us
  Pallas kernels: 0 us -> 9 us
  waiting for transfers between devices: 19 us -> 22 us
    scatter x1 -> x0, local copies, waits for them, and re-layouts: 15.5 us -> none  [on_device(): inverse = jnp.zeros((page_total,), jnp.int32).at[page_table].set(jnp.aran...]
    dot_general x4 -> x0, matrix products: 13 us -> none  [the longest x1 6.95 us: on_device(): jnp.einsum('gpqd,pgtd->pgqt', page_query, key_cache, preferred_element_ty...]
    all_to_all x3 -> x2, starting transfers between devices: 28.7 us -> 17.5 us  [the longest x1 11.5 us: on_device(): lax.all_to_all(jnp.broadcast_to(mine[None], (devices, rows, head_width)),...]
    pallas_call x0 -> x2, Pallas kernels: none -> 9 us  [the longest x1 8.01 us: on_device(): pl.pallas_call(lambda *refs: attend_kernel(scale2, *refs), out_shape=jax....]
    gather x5 -> x0, local copies, waits for them, and re-layouts: 4.77 us -> none  [the longest x1 1.43 us: on_device(): in_cache = (positions < (lengths[page_seq] - 1)[:, None])[:, None, None, :]]
    all_to_all x3 -> x2, waiting for transfers between devices: 19 us -> 22 us  [the longest x1 14.8 us: on_device(): received = lax.all_to_all(sent, 'kv', 0, 0, tiled=True)]
    transpose x5 -> x0, local copies, waits for them, and re-layouts: 1.8 us -> none  [the longest x1 1.31 us: split_up(): return jnp.moveaxis(pieces, dim, 0)]
    reduce_sum x3 -> x5, other arithmetic: 1.06 us -> 2.61 us  [the longest x1 0.99 us: plan_pages(): jnp.sum(jnp.where(hit, jnp.arange(total, dtype=jnp.int32)[None, :], 0), a...]
  transfers between devices with their start and end apart: 3 -> 2, of which waited for: 2 -> 2; matrix products, arithmetic and copies ran while one was open for 30% -> 5% of each run, Pallas kernels for 0% -> 0%
where the time goes in v1:
time: 53.9 us; the launch traced here: 53.4 us
  waiting for transfers between devices  22 us (41%)
  starting transfers between devices  17.5 us (32%)
  Pallas kernels  9 us (17%)
  other arithmetic  2.64 us (5%)
  local copies, waits for them, and re-layouts  1.44 us (3%)
  between operations  0.78 us (1%)
    all_to_all x1, waiting for transfers between devices, on_device(): received = lax.all_to_all(sent, 'kv', 0, 0, tiled=True)  14.8 us
    all_to_all x1, starting transfers between devices, on_device(): lax.all_to_all(jnp.broadcast_to(mine[None], (devices, rows, head_width)),...  11.5 us
    pallas_call x1, Pallas kernels, on_device(): pl.pallas_call(lambda *refs: attend_kernel(scale2, *refs), out_shape=jax....  8.01 us
    all_to_all x1, waiting for transfers between devices, on_device(): lax.all_to_all(jnp.broadcast_to(mine[None], (devices, rows, head_width)),...  7.17 us
    all_to_all x1, starting transfers between devices, on_device(): received = lax.all_to_all(sent, 'kv', 0, 0, tiled=True)  5.97 us
    broadcast_in_dim x1, local copies, waits for them, and re-layouts, on_device(): jnp.broadcast_to(mine[None], (devices, rows, head_width))  1.41 us
  transfers between devices with their start and end apart: 2, of which 2 were waited for; matrix products, arithmetic and copies ran while one was open for 5% of the time, Pallas kernels for 0%

profile of v1, /device:TPU:0, one launch (start us, length us, event | category | flops | bytes accessed | tf_op | source)
XLA Modules:
  0.0 53.4 jit_solution(5447857293269891624)
XLA Ops:
  0.0 1.4 %broadcast_in_dim.75 = bf16[64,16,128]{2,1,0:T(8,128)(2,1)} broadcast(bf16[16,128]{1,0:T(8,128)(2,1)} %bitcast.2), dimensions={1,2} | broadcast | bytes 266240 | tf_op jit(solution)/shard_map/broadcast_in_dim | solution.py:212
  1.4 11.5 %all-to-all-start = ((bf16[64,16,128]{2,1,0:T(8,128)(2,1)}), bf16[64,16,128]{2,1,0:T(8,128)(2,1)S(1)}, u32[]{:S(2)}, u32[]{:S(2)}) async-start(bf16[64,16,128]{2,1,0:T(8,128)(2,1)} %broadcast_in_dim.75), calls=%async_computation | async-start | bytes 524288 | tf_op jit(solution)/shard_map/all_to_all | solution.py:211
  13.0 1.0 %select_reduce_fusion = s32[64]{0:T(128)S(1)} fusion(s32[4096]{0:T(1024)} %param.13, s32[64]{0:T(128)S(1)} %iota_add_fusion), kind=kLoop, calls=%fused_computation | loop fusion | flops 786368 | bytes 16896 | tf_op jit(solution)/shard_map/reduce_sum | solution.py:184
  14.0 0.8 %select_reduce_fusion.3 = s32[64]{0:T(128)S(1)} fusion(s32[32]{0:T(128)} %param.12, s32[64]{0:T(128)S(1)} %and_select_fusion.1), kind=kLoop, calls=%fused_computation.7 | loop fusion | flops 6080 | bytes 640 | tf_op jit(solution)/shard_map/reduce_sum | solution.py:187
  14.7 0.6 %select_reduce_fusion.4 = (s32[]{:T(128)}, s32[64]{0:T(128)S(1)}) fusion(s32[64]{0:T(128)S(1)} %select_reduce_fusion, s32[64]{0:T(128)S(1)} %select_reduce_fusion.3), kind=kLoop, calls=%fused_computation.16 | loop fusion | flops 1151 | bytes 772 | tf_op jit(solution)/shard_map/reduce_sum | solution.py:194
  16.1 0.1 select_reduce_fusion.2
  16.2 0.1 select_reduce_fusion.1
  16.3 0.0 copy-start
  16.3 0.0 copy-start.1
  16.3 0.0 copy-start.2
  16.3 7.2 %all-to-all-done.refs_1_ = bf16[64,16,128]{2,1,0:T(8,128)(2,1)S(1)} async-done(((bf16[64,16,128]{2,1,0:T(8,128)(2,1)}), bf16[64,16,128]{2,1,0:T(8,128)(2,1)S(1)}, u32[]{:S(2)}, u32[]{:S(2)}) %all-to-all-start) | async-done | bytes 262176 | tf_op jit(solution)/shard_map/all_to_all | solution.py:211
  23.5 8.0 %attend.1 = f32[64,24,128]{2,1,0:T(8,128)} custom-call(s32[128]{0:T(128)S(1)} %concatenate.3.refs_0_, bf16[64,16,128]{2,1,0:T(8,128)(2,1)S(1)} %all-to-all-done.refs_1_, bf16[64,4,128,128]{3,2,1,0:T(8,128)(2,1)} %refs_2_.1, bf16[64,4,128,128]{3,2,1,0:T(8,128)(2,1)} %refs_3_.2), custom_call_target="tpu_custom_call" | custom-call | tf_op jit(solution)/shard_map/attend/pallas_call | solution.py:222
  31.5 6.0 %all-to-all-start.1 = ((f32[64,24,128]{2,1,0:T(8,128)}), f32[64,24,128]{2,1,0:T(8,128)S(1)}, u32[]{:S(2)}, u32[]{:S(2)}) async-start(f32[64,24,128]{2,1,0:T(8,128)} %attend.1), calls=%async_computation.1 | async-start | bytes 1572864 | tf_op jit(solution)/shard_map/all_to_all | solution.py:244
  37.5 14.8 %all-to-all-done.1.refs_1_ = f32[64,24,128]{2,1,0:T(8,128)S(1)} async-done(((f32[64,24,128]{2,1,0:T(8,128)}), f32[64,24,128]{2,1,0:T(8,128)S(1)}, u32[]{:S(2)}, u32[]{:S(2)}) %all-to-all-start.1) | async-done | bytes 786464 | tf_op jit(solution)/shard_map/all_to_all | solution.py:244
  52.4 0.0 copy-done
  52.4 0.0 copy-done.1
  52.4 0.0 copy-done.2
  52.4 1.0 %merge.1 = bf16[4,4,128]{2,1,0:T(4,128)(2,1)} custom-call(s32[1]{0:T(128)} %bitcast.refs_0_, f32[64,24,128]{2,1,0:T(8,128)S(1)} %all-to-all-done.1.refs_1_, bf16[16,128]{1,0:T(8,128)(2,1)S(1)} %bitcast.3, bf16[32,4,128]{2,1,0:T(4,128)(2,1)S(1)} %copy-done, bf16[32,4,128]{2,1,0:T(4,128)(2,1)S(1)} %copy-done.1), custom_call_target="tpu_custom_call" | custom-call | tf_op jit(solution)/shard_map/merge/pallas_call | solution.py:246
  (5 shorter events, 0.0 us)
Async XLA Ops:
  1.4 22.1 %all-to-all-start = ((bf16[64,16,128]{2,1,0:T(8,128)(2,1)}), bf16[64,16,128]{2,1,0:T(8,128)(2,1)S(1)}, u32[]{:S(2)}, u32[]{:S(2)}) async-start(bf16[64,16,128]{2,1,0:T(8,128)(2,1)} %broadcast_in_dim.75), calls=%async_computation | async-start | bytes 524288 | tf_op jit(solution)/shard_map/all_to_all | solution.py:211
  16.3 36.1 %copy-start = (bf16[32,4,128]{2,1,0:T(4,128)(2,1)S(1)}, bf16[32,4,128]{2,1,0:T(4,128)(2,1)}, u32[]{:S(2)}) copy-start(bf16[32,4,128]{2,1,0:T(4,128)(2,1)} %refs_3_.3) | copy-start | bytes 98308
  16.3 36.1 %copy-start.1 = (bf16[32,4,128]{2,1,0:T(4,128)(2,1)S(1)}, bf16[32,4,128]{2,1,0:T(4,128)(2,1)}, u32[]{:S(2)}) copy-start(bf16[32,4,128]{2,1,0:T(4,128)(2,1)} %refs_4_.1) | copy-start | bytes 98308
  16.3 36.0 %copy-start.2 = (bf16[4,4,128]{2,1,0:T(4,128)(2,1)S(1)}, bf16[4,4,128]{2,1,0:T(4,128)(2,1)}, u32[]{:S(2)}) copy-start(bf16[4,4,128]{2,1,0:T(4,128)(2,1)} %param.7) | copy-start | bytes 12292
  31.5 20.8 %all-to-all-start.1 = ((f32[64,24,128]{2,1,0:T(8,128)}), f32[64,24,128]{2,1,0:T(8,128)S(1)}, u32[]{:S(2)}, u32[]{:S(2)}) async-start(f32[64,24,128]{2,1,0:T(8,128)} %attend.1), calls=%async_computation.1 | async-start | bytes 1572864 | tf_op jit(solution)/shard_map/all_to_all | solution.py:244

commit v2 on v1

--- a/solution.py
+++ b/solution.py
@@ -9,6 +9,7 @@
 
 LOWEST = -1e30
 GROUP = 8
+FIRST = 42
 MIB = 1024 * 1024
 
 
@@ -28,13 +29,14 @@
     def seq_of(i):
         return (plan_ref[i] // pages) & (seqs - 1)
 
-    def copy(hbm, vmem, sem, i):
-        return pltpu.make_async_copy(hbm.at[page_of(i)], vmem.at[i], sem.at[i])
+    def copy(hbm, vmem, sem, g, u):
+        i = g * GROUP + u
+        return pltpu.make_async_copy(hbm.at[page_of(i)], vmem.at[i], sem.at[g])
 
     def start(hbm, vmem, sem):
         def some(g, _):
             for u in range(GROUP):
-                copy(hbm, vmem, sem, g * GROUP + u).start()
+                copy(hbm, vmem, sem, g, u).start()
             return 0
 
         lax.fori_loop(0, groups, some, 0)
@@ -49,7 +51,7 @@
     def regroup(s, _):
         for h in range(2):
             for j in range(pairs):
-                q_ref[s, j, 8 * h : 8 * h + 8] = arrived_ref[2 * s + h, 8 * j : 8 * j + 8]
+                q_ref[s, j, 8 * h : 8 * h + 8] = arrived_ref[(2 * s + h - FIRST) % (2 * seqs), 8 * j : 8 * j + 8]
         return 0
 
     lax.fori_loop(0, seqs, regroup, 0, unroll=4)
@@ -59,7 +61,8 @@
             body(g * GROUP + u)
 
     def wait_for(hbm, vmem, sem, g):
-        each(g, lambda i: copy(hbm, vmem, sem, i).wait())
+        part = pl.ds(g * GROUP, GROUP)
+        pltpu.make_async_copy(hbm.at[pl.ds(0, GROUP)], vmem.at[part], sem.at[g]).wait()
 
     def score(i):
         s = seq_of(i)
@@ -117,28 +120,67 @@
     staged(k_hbm, k_ref, k_sem, score, weigh)
     staged(v_hbm, v_ref, v_sem, combine, gather)
 
+    kind = token % 4
+    left = token < 4
+
     def pack(s, _):
         for h in range(2):
+            to = (2 * s + h - FIRST) % (2 * seqs)
             note = jnp.zeros((8, 128), jnp.float32)
             for j in range(pairs):
-                send_ref[2 * s + h, 8 * j : 8 * j + 8] = out_ref[s, j, h]
+                send_ref[to, 2 * j] = out_ref[s, j, h][:4]
+                send_ref[to, 2 * j + 1] = out_ref[s, j, h][4:]
                 total = jnp.sum(sum_ref[s, j, h], axis=1, keepdims=True)
-                note = jnp.where(token == j, max_ref[s, j, h], note)
-                note = jnp.where(token == pairs + j, total, note)
-            send_ref[2 * s + h, 8 * pairs :] = note
+                note = jnp.where(kind == j, max_ref[s, j, h], note)
+                note = jnp.where(kind == pairs + j, total, note)
+            send_ref[to, 2 * pairs] = jnp.where(left, note, pltpu.roll(note, 4, 0))[:4]
         return 0
 
     lax.fori_loop(0, seqs, pack, 0, unroll=4)
 
 
-def merge_kernel(scale2, seq_ref, recv_ref, q_ref, k_ref, v_ref, o_ref):
+def attend(plan, arrived, key_cache, value_cache):
+    pages_here, kv_here, page_len, head_width = key_cache.shape
+    devices, rows, _ = arrived.shape
+    seq_count, pairs = devices // 2, kv_here // 2
+    scale2 = math.log2(math.e) / math.sqrt(head_width)
+    vmem = pl.BlockSpec(memory_space=pltpu.VMEM)
+    smem = pl.BlockSpec(memory_space=pltpu.SMEM)
+    hbm = pl.BlockSpec(memory_space=pltpu.HBM)
+    by_page = pltpu.VMEM((pages_here, pairs, 2, 8, 128), jnp.float32)
+    by_seq = pltpu.VMEM((seq_count, pairs, 2, 8, 128), jnp.float32)
+    cached = pltpu.VMEM(key_cache.shape, jnp.bfloat16)
+    return pl.pallas_call(
+        lambda *refs: attend_kernel(scale2, *refs),
+        out_shape=jax.ShapeDtypeStruct((devices, kv_here + 1, rows // kv_here, head_width), jnp.float32),
+        in_specs=[smem, vmem, hbm, hbm],
+        out_specs=vmem,
+        scratch_shapes=[
+            cached,
+            cached,
+            pltpu.VMEM((seq_count, pairs, 16, head_width), jnp.bfloat16),
+            by_page,
+            by_page,
+            by_page,
+            by_seq,
+            by_seq,
+            by_seq,
+            pltpu.SemaphoreType.DMA((pages_here // GROUP,)),
+            pltpu.SemaphoreType.DMA((pages_here // GROUP,)),
+        ],
+        name="attend",
+        compiler_params=pltpu.CompilerParams(vmem_limit_bytes=52 * MIB),
+    )(plan, arrived, key_cache, value_cache)
+
+
+def merge_kernel(scale2, recv_ref, q_ref, k_ref, v_ref, o_ref, note_ref):
     sources = recv_ref.shape[0]
     pairs = q_ref.shape[0] // 8
+    notes = 2 * pairs
     lane = lax.broadcasted_iota(jnp.int32, (8, 128), 1)
     upper = lax.broadcasted_iota(jnp.int32, (8, 128), 0) < 4
-    s = seq_ref[0]
-    keys = k_ref[s].astype(jnp.float32)
-    fresh = v_ref[s].astype(jnp.float32)
+    keys = k_ref[...].astype(jnp.float32)
+    fresh = v_ref[...].astype(jnp.float32)
     query = q_ref[...].astype(jnp.float32)
 
     def spread(x, j):
@@ -152,7 +194,10 @@
         new = jnp.where(lane == j, score, new)
     top = new
     for d in range(sources):
-        top = jnp.maximum(top, recv_ref[d, 8 * pairs :])
+        part = recv_ref[d, 2 * pairs]
+        note = jnp.concatenate([part, pltpu.roll(part, 128 - notes, 1)], axis=0)
+        note_ref[d] = note
+        top = jnp.maximum(top, note)
     top = jnp.where(lane < pairs, top, 0.0)
     fresh_weight = jnp.where(lane < pairs, jnp.exp2((new - top) * scale2), 0.0)
     totals = [jnp.zeros((8, 128), jnp.float32) for _ in range(pairs)]
@@ -161,15 +206,16 @@
     for j in range(pairs):
         outs.append(weights[j] * spread(fresh, j))
     for d in range(sources):
-        note = recv_ref[d, 8 * pairs :]
+        note = note_ref[d]
         weight = jnp.exp2(jnp.where(lane < pairs, note - top, 0.0) * scale2)
         for j in range(pairs):
             w = jnp.broadcast_to(weight[:, j : j + 1], (8, 128))
             totals[j] = totals[j] + w * note
-            outs[j] = outs[j] + w * recv_ref[d, 8 * j : 8 * j + 8]
+            part = jnp.concatenate([recv_ref[d, 2 * j], recv_ref[d, 2 * j + 1]], axis=0)
+            outs[j] = outs[j] + w * part
     for j in range(pairs):
         at = pairs + j
-        total = totals[j][:, at : at + 1] + weights[j][:, at : at + 1]
+        total = totals[j][:, at : at + 1] + weights[j][:, at - pairs : at - pairs + 1]
         done = (outs[j] / total).astype(o_ref.dtype)
         o_ref[2 * j] = done[:4]
         o_ref[2 * j + 1] = done[4:]
@@ -196,6 +242,12 @@
     return jnp.concatenate([order, jnp.broadcast_to(groups, (pages,))])
 
 
+def exchange(x):
+    devices = x.shape[0]
+    order = [(d + FIRST) % devices for d in range(devices)]
+    return lax.all_to_all(x, "kv", 0, 0, tiled=True, axis_index_groups=[order])
+
+
 def on_device(queries, key_cache, value_cache, key_new, value_new, lengths, page_table):
     kv_here, local_rows, head_width = queries.shape
     pages_here = key_cache.shape[0]
@@ -208,49 +260,27 @@
     kv_index = lax.axis_index("kv")
 
     mine = queries.reshape(rows, head_width)
-    arrived = lax.all_to_all(
-        jnp.broadcast_to(mine[None], (devices, rows, head_width)), "kv", 0, 0, tiled=True
-    )
+    arrived = exchange(jnp.broadcast_to(mine[None], (devices, rows, head_width)))
     plan = plan_pages(kv_index, pages_here, page_len, lengths, page_table)
+    own = kv_index * local_rows // (devices * local_rows // seq_count)
+    fresh_key = lax.dynamic_index_in_dim(key_new, own, 0, keepdims=False)
+    fresh_value = lax.dynamic_index_in_dim(value_new, own, 0, keepdims=False)
+    plan, fresh_key, fresh_value = lax.optimization_barrier((plan, fresh_key, fresh_value))
+
+    sent = attend(plan, arrived, key_cache, value_cache)
 
     vmem = pl.BlockSpec(memory_space=pltpu.VMEM)
-    smem = pl.BlockSpec(memory_space=pltpu.SMEM)
-    hbm = pl.BlockSpec(memory_space=pltpu.HBM)
-    by_page = pltpu.VMEM((pages_here, pairs, 2, 8, 128), jnp.float32)
-    by_seq = pltpu.VMEM((seq_count, pairs, 2, 8, 128), jnp.float32)
-    cached = pltpu.VMEM(key_cache.shape, jnp.bfloat16)
-    sent = pl.pallas_call(
-        lambda *refs: attend_kernel(scale2, *refs),
-        out_shape=jax.ShapeDtypeStruct((devices, rows + 8, head_width), jnp.float32),
-        in_specs=[smem, vmem, hbm, hbm],
-        out_specs=vmem,
-        scratch_shapes=[
-            cached,
-            cached,
-            pltpu.VMEM((seq_count, pairs, 16, head_width), jnp.bfloat16),
-            by_page,
-            by_page,
-            by_page,
-            by_seq,
-            by_seq,
-            by_seq,
-            pltpu.SemaphoreType.DMA((pages_here,)),
-            pltpu.SemaphoreType.DMA((pages_here,)),
-        ],
-        name="attend",
-        compiler_params=pltpu.CompilerParams(vmem_limit_bytes=52 * MIB),
-    )(plan, arrived, key_cache, value_cache)
-
-    received = lax.all_to_all(sent, "kv", 0, 0, tiled=True)
+    received = exchange(sent)
 
     return pl.pallas_call(
         lambda *refs: merge_kernel(scale2, *refs),
         out_shape=jax.ShapeDtypeStruct(queries.shape, jnp.bfloat16),
-        in_specs=[smem, vmem, vmem, vmem, vmem],
+        in_specs=[vmem] * 4,
         out_specs=vmem,
+        scratch_shapes=[pltpu.VMEM((devices, 8, head_width), jnp.float32)],
         name="merge",
         compiler_params=pltpu.CompilerParams(vmem_limit_bytes=8 * MIB),
-    )((kv_index // 2).reshape(1).astype(jnp.int32), received, mine, key_new, value_new)
+    )(received, mine, fresh_key, fresh_value)
 
 
 def solution(mesh):

time: 53.9 us -> 45.3 us (0.84)
  waiting for transfers between devices: 22 us -> 0.01 us
  blocking collectives: 0 us -> 17.7 us
  starting transfers between devices: 17.5 us -> 13.9 us
  Pallas kernels: 9 us -> 7.64 us
  local copies, waits for them, and re-layouts: 1.44 us -> 2.13 us
    all_to_all x2 -> x1, waiting for transfers between devices: 22 us -> 0.01 us  [exchange(): return lax.all_to_all(x, 'kv', 0, 0, tiled=True, axis_index_groups=[order])]
    all_to_all x0 -> x1, blocking collectives: none -> 17.7 us  [exchange(): return lax.all_to_all(x, 'kv', 0, 0, tiled=True, axis_index_groups=[order])]
    all_to_all x2 -> x1, starting transfers between devices: 17.5 us -> 13.9 us  [exchange(): return lax.all_to_all(x, 'kv', 0, 0, tiled=True, axis_index_groups=[order])]
    pallas_call x1, Pallas kernels: 8.01 us -> 6.52 us  [attend(): pl.pallas_call(lambda *refs: attend_kernel(scale2, *refs), out_shape=jax....]
    squeeze x0 -> x1, local copies, waits for them, and re-layouts: none -> 0.71 us  [on_device(): fresh_value = lax.dynamic_index_in_dim(value_new, own, 0, keepdims=False)]
  transfers between devices with their start and end apart: 2 -> 1, of which waited for: 2 -> 0; matrix products, arithmetic and copies ran while one was open for 5% -> 7% of each run, Pallas kernels for 0% -> 0%
where the time goes in v2:
time: 45.3 us; the launch traced here: 44.8 us
  blocking collectives  17.7 us (39%)
  starting transfers between devices  13.9 us (31%)
  Pallas kernels  7.64 us (17%)
  other arithmetic  2.63 us (6%)
  local copies, waits for them, and re-layouts  2.13 us (5%)
  between operations  0.76 us (2%)
    all_to_all x1, blocking collectives, exchange(): return lax.all_to_all(x, 'kv', 0, 0, tiled=True, axis_index_groups=[order])  17.7 us
    all_to_all x1, starting transfers between devices, exchange(): return lax.all_to_all(x, 'kv', 0, 0, tiled=True, axis_index_groups=[order])  13.9 us
    pallas_call x1, Pallas kernels, attend(): pl.pallas_call(lambda *refs: attend_kernel(scale2, *refs), out_shape=jax....  6.52 us
    broadcast_in_dim x1, local copies, waits for them, and re-layouts, on_device(): jnp.broadcast_to(mine[None], (devices, rows, head_width))  1.41 us
    pallas_call x1, Pallas kernels, on_device(): pl.pallas_call(lambda *refs: merge_kernel(scale2, *refs), out_shape=jax.S...  1.12 us
    reduce_sum x1, other arithmetic, plan_pages(): jnp.sum(jnp.where(hit, jnp.arange(total, dtype=jnp.int32)[None, :], 0), a...  0.99 us
  transfers between devices with their start and end apart: 1, of which 0 were waited for; matrix products, arithmetic and copies ran while one was open for 7% of the time, Pallas kernels for 0%

profile of v2, /device:TPU:0, one launch (start us, length us, event | category | flops | bytes accessed | tf_op | source)
XLA Modules:
  0.0 44.8 jit_solution(6443186638157089436)
XLA Ops:
  0.0 1.4 %broadcast_in_dim.75 = bf16[64,16,128]{2,1,0:T(8,128)(2,1)} broadcast(bf16[16,128]{1,0:T(8,128)(2,1)} %bitcast.5), dimensions={1,2} | broadcast | bytes 266240 | tf_op jit(solution)/shard_map/broadcast_in_dim | solution.py:263
  1.4 13.9 %all-to-all-start = ((bf16[64,16,128]{2,1,0:T(8,128)(2,1)}), bf16[64,16,128]{2,1,0:T(8,128)(2,1)S(1)}, u32[]{:S(2)}, u32[]{:S(2)}) async-start(bf16[64,16,128]{2,1,0:T(8,128)(2,1)} %broadcast_in_dim.75), calls=%async_computation | async-start | bytes 524288 | tf_op jit(solution)/shard_map/all_to_all | solution.py:248
  15.4 1.0 %select_reduce_fusion = s32[64]{0:T(128)S(1)} fusion(s32[4096]{0:T(1024)} %param.13, s32[64]{0:T(128)S(1)} %iota_add_fusion), kind=kLoop, calls=%fused_computation | loop fusion | flops 786368 | bytes 16896 | tf_op jit(solution)/shard_map/reduce_sum | solution.py:230
  16.4 0.8 %select_reduce_fusion.3 = s32[64]{0:T(128)S(1)} fusion(s32[32]{0:T(128)} %param.12, s32[64]{0:T(128)S(1)} %and_select_fusion.1), kind=kLoop, calls=%fused_computation.7 | loop fusion | flops 6080 | bytes 640 | tf_op jit(solution)/shard_map/reduce_sum | solution.py:233
  17.1 0.6 %select_reduce_fusion.4 = (s32[]{:T(128)}, s32[64]{0:T(128)S(1)}) fusion(s32[64]{0:T(128)S(1)} %select_reduce_fusion, s32[64]{0:T(128)S(1)} %select_reduce_fusion.3), kind=kLoop, calls=%fused_computation.18 | loop fusion | flops 1151 | bytes 772 | tf_op jit(solution)/shard_map/reduce_sum | solution.py:240
  17.8 0.1 select_reduce_fusion.2
  18.6 0.1 select_reduce_fusion.1
  18.7 0.7 %dynamic-slice_bitcast_fusion = (bf16[4,128]{1,0:T(4,128)(2,1)S(1)}, bf16[4,128]{1,0:T(4,128)(2,1)S(1)}) fusion(bf16[32,4,128]{2,1,0:T(4,128)(2,1)} %param.11, s32[]{:T(128)S(6)} %select_n.68, bf16[32,4,128]{2,1,0:T(4,128)(2,1)} %param.10), kind=kLoop, calls=%fused_computation.14 | loop fusion | bytes 4100 | tf_op jit(solution)/shard_map/jit(dynamic_index_in_dim)/squeeze | solution.py:267
  19.4 0.0 copy-start
  19.4 0.0 all-to-all-done.refs_1_
  19.4 6.5 %attend.1 = f32[64,5,4,128]{3,2,1,0:T(4,128)S(1)} custom-call(s32[128]{0:T(128)S(1)} %concatenate.3.refs_0_, bf16[64,16,128]{2,1,0:T(8,128)(2,1)S(1)} %all-to-all-done.refs_1_, bf16[64,4,128,128]{3,2,1,0:T(8,128)(2,1)} %refs_2_.1, bf16[64,4,128,128]{3,2,1,0:T(8,128)(2,1)} %refs_3_.1), custom_call_target="tpu_custom_call" | custom-call | tf_op jit(solution)/shard_map/attend/pallas_call | solution.py:153
  26.0 17.7 %all_to_all.10.refs_0_ = f32[64,5,4,128]{3,2,1,0:T(4,128)S(1)} all-to-all(f32[64,5,4,128]{3,2,1,0:T(4,128)S(1)} %attend.1), channel_id=1, replica_groups={{84,86,88,90,92,94,96,98,100,102,104,106,108,110,112,114,116,118,120,12..., dimensions={0} | all-to-all | bytes 1310720 | tf_op jit(solution)/shard_map/all_to_all | solution.py:248
  43.7 0.0 copy-done
  43.7 1.1 %merge.1 = bf16[4,4,128]{2,1,0:T(4,128)(2,1)} custom-call(f32[64,5,4,128]{3,2,1,0:T(4,128)S(1)} %all_to_all.10.refs_0_, bf16[16,128]{1,0:T(8,128)(2,1)S(1)} %bitcast.6, bf16[4,128]{1,0:T(4,128)(2,1)S(1)} %get-tuple-element.9.refs_2_, bf16[4,128]{1,0:T(4,128)(2,1)S(1)} %get-tuple-element.10.refs_3_), custom_call_target="tpu_custom_call" | custom-call | tf_op jit(solution)/shard_map/merge/pallas_call | solution.py:275
  (5 shorter events, 0.0 us)
Async XLA Ops:
  1.4 18.0 %all-to-all-start = ((bf16[64,16,128]{2,1,0:T(8,128)(2,1)}), bf16[64,16,128]{2,1,0:T(8,128)(2,1)S(1)}, u32[]{:S(2)}, u32[]{:S(2)}) async-start(bf16[64,16,128]{2,1,0:T(8,128)(2,1)} %broadcast_in_dim.75), calls=%async_computation | async-start | bytes 524288 | tf_op jit(solution)/shard_map/all_to_all | solution.py:248
  19.4 24.2 %copy-start = (bf16[4,4,128]{2,1,0:T(4,128)(2,1)S(1)}, bf16[4,4,128]{2,1,0:T(4,128)(2,1)}, u32[]{:S(2)}) copy-start(bf16[4,4,128]{2,1,0:T(4,128)(2,1)} %param.7) | copy-start | bytes 12292

commit v3 on v2

v3 whole, which is shorter than its diff:
```python
import math

import jax
import jax.numpy as jnp
from jax import lax
from jax.experimental import pallas as pl
from jax.experimental.pallas import tpu as pltpu
from jax.sharding import PartitionSpec as P

LOWEST = -1e30
SCORE_UNIT = 1.0 / 8.0
NO_SCORE = -480000.0
MOST_POWER = 120.0
GROUP = 8
QUERY_FIRST = 42
RESULT_FIRST = 42
MIB = 1024 * 1024


def attend_kernel(
    scale2, plan_ref, arrived_ref, k_hbm, v_hbm, send_ref,
    list_ref, k_ref, v_ref, q_ref, score_ref, prob_ref, pmax_ref, max_ref, sum_ref, out_ref, k_sem, v_sem,
):
    pages = k_ref.shape[0]
    seqs, pairs = q_ref.shape[0], q_ref.shape[1]
    token = lax.broadcasted_iota(jnp.int32, (8, 128), 1)
    upper = lax.broadcasted_iota(jnp.int32, (8, 128), 0) < 4

    def page_of(i):
        return list_ref[i] & (pages - 1)

    def seq_of(i):
        return (list_ref[i] // pages) & (seqs - 1)

    def start(hbm, vmem, sem, i):
        pltpu.make_async_copy(hbm.at[page_of(i)], vmem.at[i], sem.at[i // GROUP]).start()

    def find(p, count):
        code = plan_ref[0, p]
        used = code >= seqs
        list_ref[count] = code * pages + p

        @pl.when(used)
        def _():
            start(k_hbm, k_ref, k_sem, count)

        return count + used.astype(jnp.int32)

    count = lax.fori_loop(0, pages, find, 0, unroll=4)
    groups = jnp.maximum((count + GROUP - 1) // GROUP, 1)

    def pad(i, _):
        list_ref[i] = 0
        start(k_hbm, k_ref, k_sem, i)
        return 0

    lax.fori_loop(count, groups * GROUP, pad, 0)

    def rest(g, _):
        for u in range(GROUP):
            start(v_hbm, v_ref, v_sem, g * GROUP + u)
        return 0

    lax.fori_loop(0, groups, rest, 0)

    max_ref[...] = jnp.full(max_ref.shape, LOWEST, jnp.float32)
    sum_ref[...] = jnp.zeros(sum_ref.shape, jnp.float32)
    out_ref[...] = jnp.zeros(out_ref.shape, jnp.float32)

    def regroup(s, _):
        for h in range(2):
            for j in range(pairs):
                q_ref[s, j, 8 * h : 8 * h + 8] = arrived_ref[(2 * s + h - QUERY_FIRST) % (2 * seqs), 8 * j : 8 * j + 8]
        return 0

    lax.fori_loop(0, seqs, regroup, 0, unroll=4)

    def each(g, body):
        for u in range(GROUP):
            body(g * GROUP + u)

    def wait_for(hbm, vmem, sem, g):
        part = pl.ds(g * GROUP, GROUP)
        pltpu.make_async_copy(hbm.at[pl.ds(0, GROUP)], vmem.at[part], sem.at[g]).wait()

    def score(i):
        s = seq_of(i)
        for j in range(pairs):
            keys = k_ref[i, 2 * j : 2 * j + 2].reshape(256, 128)
            both = lax.dot_general(
                q_ref[s, j], keys, (((1,), (1,)), ((), ())), preferred_element_type=jnp.float32
            )
            for h in range(2):
                rows = slice(8 * h, 8 * h + 8)
                score_ref[i, j, h] = jnp.where(upper, both[rows, :128], both[rows, 128:])

    def weigh(i):
        s = seq_of(i)
        inside = token < list_ref[i] // (pages * seqs)
        for j in range(pairs):
            for h in range(2):
                score = jnp.where(inside, score_ref[i, j, h], LOWEST)
                top = jnp.max(score, axis=1, keepdims=True)
                prob_ref[i, j, h] = jnp.where(inside, jnp.exp2((score - top) * scale2), 0.0)
                top = jnp.broadcast_to(top, (8, 128))
                pmax_ref[i, j, h] = top
                max_ref[s, j, h] = jnp.maximum(max_ref[s, j, h], top)

    def combine(i):
        for j in range(pairs):
            probs = jnp.concatenate([prob_ref[i, j, 0], prob_ref[i, j, 1]], axis=0)
            values = jnp.concatenate([v_ref[i, 2 * j], v_ref[i, 2 * j + 1]], axis=1)
            both = jnp.dot(probs.astype(jnp.bfloat16), values, preferred_element_type=jnp.float32)
            for h in range(2):
                rows = slice(8 * h, 8 * h + 8)
                score_ref[i, j, h] = jnp.where(upper, both[rows, :128], both[rows, 128:])

    def gather(i):
        s = seq_of(i)
        for j in range(pairs):
            for h in range(2):
                factor = jnp.exp2((pmax_ref[i, j, h] - max_ref[s, j, h]) * scale2)
                sum_ref[s, j, h] = sum_ref[s, j, h] + factor * prob_ref[i, j, h]
                out_ref[s, j, h] = out_ref[s, j, h] + factor * score_ref[i, j, h]

    def staged(hbm, vmem, sem, first, second):
        wait_for(hbm, vmem, sem, 0)
        each(0, first)

        def step(g, _):
            wait_for(hbm, vmem, sem, g)
            each(g - 1, second)
            each(g, first)
            return 0

        lax.fori_loop(1, groups, step, 0)
        each(groups - 1, second)

    staged(k_hbm, k_ref, k_sem, score, weigh)
    staged(v_hbm, v_ref, v_sem, combine, gather)

    kind = token & 3
    first = (token & 4) == 0
    block = lax.shift_right_logical(token, 3)

    def rounded(x):
        return x.astype(jnp.bfloat16).astype(jnp.float32)

    def pack(s, _):
        for h in range(2):
            to = (2 * s + h - RESULT_FIRST) & (2 * seqs - 1)
            note = jnp.zeros((8, 128), jnp.float32)
            powers = jnp.zeros((8, 128), jnp.float32)
            for j in range(pairs):
                out = out_ref[s, j, h]
                largest = jnp.max(jnp.abs(out), axis=1, keepdims=True)
                power = jnp.clip(jnp.ceil(-jnp.log2(largest)), 0.0, MOST_POWER)
                out = out * jnp.exp2(power)
                send_ref[to, 2 * j] = out[:4]
                send_ref[to, 2 * j + 1] = out[4:]
                total = jnp.sum(sum_ref[s, j, h], axis=1, keepdims=True)
                best = jnp.maximum(max_ref[s, j, h], NO_SCORE) * SCORE_UNIT
                note = jnp.where(kind == j, best, note)
                note = jnp.where(kind == pairs + j, total, note)
                powers = jnp.where(kind == j, power, powers)
            note = jnp.where(first, note, pltpu.roll(note, 4, 0))
            powers = jnp.where(first, powers, pltpu.roll(powers, 4, 0))
            high = rounded(note)
            middle = rounded(note - high)
            low = note - high - middle
            note = jnp.where(block == 0, high, jnp.where(block == 1, middle, low))
            send_ref[to, 2 * pairs] = jnp.where(block < 3, note, powers)[:4]
        return 0

    lax.fori_loop(0, seqs, pack, 0, unroll=4)


def attend(plan, arrived, key_cache, value_cache):
    pages_here, kv_here, page_len, head_width = key_cache.shape
    devices, rows, _ = arrived.shape
    seq_count, pairs = devices // 2, kv_here // 2
    scale2 = math.log2(math.e) / math.sqrt(head_width)
    vmem = pl.BlockSpec(memory_space=pltpu.VMEM)
    smem = pl.BlockSpec(memory_space=pltpu.SMEM)
    hbm = pl.BlockSpec(memory_space=pltpu.HBM)
    by_page = pltpu.VMEM((pages_here, pairs, 2, 8, 128), jnp.float32)
    by_seq = pltpu.VMEM((seq_count, pairs, 2, 8, 128), jnp.float32)
    cached = pltpu.VMEM(key_cache.shape, jnp.bfloat16)
    return pl.pallas_call(
        lambda *refs: attend_kernel(scale2, *refs),
        out_shape=jax.ShapeDtypeStruct((devices, kv_here + 1, rows // kv_here, head_width), jnp.float32),
        in_specs=[smem, vmem, hbm, hbm],
        out_specs=vmem,
        scratch_shapes=[
            pltpu.SMEM((pages_here + GROUP,), jnp.int32),
            cached,
            cached,
            pltpu.VMEM((seq_count, pairs, 16, head_width), jnp.bfloat16),
            by_page,
            by_page,
            by_page,
            by_seq,
            by_seq,
            by_seq,
            pltpu.SemaphoreType.DMA((pages_here // GROUP,)),
            pltpu.SemaphoreType.DMA((pages_here // GROUP,)),
        ],
        name="attend",
        compiler_params=pltpu.CompilerParams(vmem_limit_bytes=52 * MIB),
    )(plan, arrived, key_cache, value_cache)


def merge_kernel(scale2, recv_ref, q_ref, k_ref, v_ref, o_ref):
    heads, local_rows, width = q_ref.shape
    lines = recv_ref.shape[1]
    pairs = heads // 2
    own = lax.axis_index("kv") * k_ref.shape[0] // (lines // local_rows)
    unit = scale2 / SCORE_UNIT
    notes = recv_ref[heads].astype(jnp.bfloat16)
    row = lax.broadcasted_iota(jnp.int32, (width, width), 0)

    def column(at, chosen):
        return jnp.where(((row & 7) == at) & chosen, 1.0, 0.0).astype(jnp.bfloat16)

    def picked(first, second):
        wide = jnp.concatenate([first, second], axis=1)
        both = jnp.dot(notes, wide, preferred_element_type=jnp.float32)
        return both[:, :width], both[:, width:]

    def at(g):
        return (g % 2) * 4 + g // 2

    powers = []
    for g in range(0, heads, 2):
        powers += picked(*(column(at(g + u), (row >= 24) & (row < 32)) for u in range(2)))
    keys = k_ref[own].astype(jnp.float32)
    fresh = v_ref[own].astype(jnp.float32)

    def folded(x, join):
        return join(x, pltpu.roll(x, 4, 0))

    for g in range(heads):
        best, sums = picked(column(at(g), row < 24), column(at(g) + pairs, row < 24))
        query = q_ref[g].astype(jnp.float32)
        query = jnp.concatenate([query, query], axis=0)
        new = jnp.sum(query * keys[g : g + 1], axis=1, keepdims=True) * SCORE_UNIT
        top = best[:8]
        for k in range(8, lines, 8):
            top = jnp.maximum(top, best[k : k + 8])
        top = jnp.maximum(folded(top, jnp.maximum), new)
        weight = jnp.exp2((new - top) * unit)
        total = jnp.zeros((8, width), jnp.float32)
        out = jnp.zeros((8, width), jnp.float32)
        for k in range(0, lines, 8):
            exponent = (best[k : k + 8] - top) * unit
            total = total + jnp.exp2(exponent) * sums[k : k + 8]
            out = out + jnp.exp2(exponent - powers[g][k : k + 8]) * recv_ref[g, k : k + 8]
        total = folded(total, jnp.add) + weight
        out = folded(out, jnp.add) + weight * fresh[g : g + 1]
        o_ref[g] = (out / total)[:local_rows].astype(o_ref.dtype)


def plan_kernel(pages, page_len, table_ref, lengths_ref, plan_ref):
    seqs, slots = table_ref.shape
    row = lax.broadcasted_iota(jnp.int32, (seqs, slots), 0)
    slot = lax.broadcasted_iota(jnp.int32, (seqs, slots), 1)
    square = (seqs, seqs)
    same = lax.broadcasted_iota(jnp.int32, square, 0) == lax.broadcasted_iota(jnp.int32, square, 1)
    length = jnp.sum(
        jnp.where(same, lengths_ref[...].astype(jnp.float32), 0.0), axis=1, keepdims=True
    ).astype(jnp.int32)
    inside = jnp.clip(length - 1 - slot * page_len, 0, page_len)
    code = (row + seqs * inside).astype(jnp.float32)
    local = table_ref[...] - lax.axis_index("kv") * pages
    lane = lax.broadcasted_iota(jnp.int32, (8, 128), 1)
    found = jnp.zeros((8, 128), jnp.float32)
    for p in range(pages):
        hit = jnp.where(local == p, code, 0.0)
        hit = sum(hit[8 * i : 8 * i + 8] for i in range(seqs // 8))
        found = jnp.where(lane == p, jnp.sum(hit, axis=1, keepdims=True), found)
    plan_ref[...] = jnp.sum(found, axis=0, keepdims=True).astype(jnp.int32)


def plan_pages(pages, page_len, lengths, page_table):
    seqs = lengths.shape[0]
    slots = page_table.shape[0] // seqs
    vmem = pl.BlockSpec(memory_space=pltpu.VMEM)
    return pl.pallas_call(
        lambda *refs: plan_kernel(pages, page_len, *refs),
        out_shape=jax.ShapeDtypeStruct((1, 128), jnp.int32),
        in_specs=[vmem, vmem],
        out_specs=vmem,
        name="plan",
        cost_estimate=pl.CostEstimate(flops=10**9, bytes_accessed=10**5, transcendentals=0),
        compiler_params=pltpu.CompilerParams(vmem_limit_bytes=2 * MIB),
    )(page_table.reshape(seqs, slots), lengths.reshape(1, seqs))


def exchange(x, first):
    devices = x.shape[0]
    order = [(d + first) % devices for d in range(devices)]
    return lax.all_to_all(x, "kv", 0, 0, tiled=True, axis_index_groups=[order])


def on_device(queries, key_cache, value_cache, key_new, value_new, lengths, page_table):
    kv_here, local_rows, head_width = queries.shape
    pages_here = key_cache.shape[0]
    page_len = key_cache.shape[2]
    seq_count = lengths.shape[0]
    devices = lax.axis_size("kv")
    pairs = kv_here // 2
    rows = kv_here * local_rows
    scale2 = math.log2(math.e) / math.sqrt(head_width)
    kv_index = lax.axis_index("kv")

    mine = queries.reshape(rows, head_width)
    arrived = exchange(jnp.broadcast_to(mine[None], (devices, rows, head_width)), QUERY_FIRST)
    plan = plan_pages(pages_here, page_len, lengths, page_table)
    sent = attend(plan, arrived, key_cache, value_cache)

    vmem = pl.BlockSpec(memory_space=pltpu.VMEM)
    received = exchange(sent.astype(jnp.float16), RESULT_FIRST).astype(jnp.float32)
    received = jnp.transpose(received, (1, 0, 2, 3)).reshape(kv_here + 1, devices * local_rows, head_width)

    return pl.pallas_call(
        lambda *refs: merge_kernel(scale2, *refs),
        out_shape=jax.ShapeDtypeStruct(queries.shape, jnp.bfloat16),
        in_specs=[vmem] * 4,
        out_specs=vmem,
        name="merge",
        compiler_params=pltpu.CompilerParams(vmem_limit_bytes=8 * MIB),
    )(received, queries, key_new, value_new)


def solution(mesh):
    placed = (
        P("head", "kv", None),
        P("kv", "head", None, None),
        P("kv", "head", None, None),
        P(None, "head", None),
        P(None, "head", None),
        P(),
        P(),
    )
    return jax.shard_map(
        on_device, mesh=mesh, in_specs=placed, out_specs=P("head", "kv", None), check_vma=False
    )
```

time: 45.3 us -> 41.9 us (0.925)
  blocking collectives: 17.7 us -> 14.8 us
  other arithmetic: 2.63 us -> 0.23 us
  waiting for transfers between devices: 0.01 us -> 1.68 us
  local copies, waits for them, and re-layouts: 2.13 us -> 2.92 us
  between operations: 0.76 us -> 0.1 us
    all_to_all x1, blocking collectives: 17.7 us -> 14.8 us  [exchange(): return lax.all_to_all(x, 'kv', 0, 0, tiled=True, axis_index_groups=[order])]
    reduce_sum x5 -> x0, other arithmetic: 2.6 us -> none  [the longest x1 0.99 us: plan_pages(): jnp.sum(jnp.where(hit, jnp.arange(total, dtype=jnp.int32)[None, :], 0), a...]
    all_to_all x1, waiting for transfers between devices: 0.01 us -> 1.68 us  [exchange(): return lax.all_to_all(x, 'kv', 0, 0, tiled=True, axis_index_groups=[order])]
    unnamed x2 -> x10, local copies, waits for them, and re-layouts: 0.01 us -> 1.39 us
    squeeze x1 -> x0, local copies, waits for them, and re-layouts: 0.71 us -> none  [on_device(): fresh_value = lax.dynamic_index_in_dim(value_new, own, 0, keepdims=False)]
  transfers between devices with their start and end apart: 1 -> 1, of which waited for: 0 -> 1; matrix products, arithmetic and copies ran while one was open for 7% -> 0% of each run, Pallas kernels for 0% -> 1%
where the time goes in v3:
time: 41.9 us; the launch traced here: 41.7 us
  blocking collectives  14.8 us (35%)
  starting transfers between devices  13.9 us (33%)
  Pallas kernels  8.02 us (19%)
  local copies, waits for them, and re-layouts  2.92 us (7%)
  waiting for transfers between devices  1.68 us (4%)
    all_to_all x1, blocking collectives, exchange(): return lax.all_to_all(x, 'kv', 0, 0, tiled=True, axis_index_groups=[order])  14.8 us
    all_to_all x1, starting transfers between devices, exchange(): return lax.all_to_all(x, 'kv', 0, 0, tiled=True, axis_index_groups=[order])  13.9 us
    pallas_call x1, Pallas kernels, attend(): pl.pallas_call(lambda *refs: attend_kernel(scale2, *refs), out_shape=jax....  6.68 us
    all_to_all x1, waiting for transfers between devices, exchange(): return lax.all_to_all(x, 'kv', 0, 0, tiled=True, axis_index_groups=[order])  1.68 us
    broadcast_in_dim x1, local copies, waits for them, and re-layouts, on_device(): jnp.broadcast_to(mine[None], (devices, rows, head_width))  1.42 us
    unnamed x10, local copies, waits for them, and re-layouts  1.39 us
    pallas_call x1, Pallas kernels, on_device(): pl.pallas_call(lambda *refs: merge_kernel(scale2, *refs), out_shape=jax.S...  1.08 us
  transfers between devices with their start and end apart: 1, of which 1 were waited for; matrix products, arithmetic and copies ran while one was open for 0% of the time, Pallas kernels for 1%

profile of v3, /device:TPU:0, one launch (start us, length us, event | category | flops | bytes accessed | tf_op | source)
XLA Modules:
  0.0 41.7 jit_solution(8453533646494291238)
XLA Ops:
  0.0 1.4 %broadcast_in_dim.8 = bf16[64,16,128]{2,1,0:T(8,128)(2,1)} broadcast(bf16[16,128]{1,0:T(8,128)(2,1)} %bitcast.7), dimensions={1,2} | broadcast | bytes 266240 | tf_op jit(solution)/shard_map/broadcast_in_dim | solution.py:317
  1.4 13.9 %all-to-all-start = ((bf16[64,16,128]{2,1,0:T(8,128)(2,1)}), bf16[64,16,128]{2,1,0:T(8,128)(2,1)S(1)}, u32[]{:S(2)}, u32[]{:S(2)}) async-start(bf16[64,16,128]{2,1,0:T(8,128)(2,1)} %broadcast_in_dim.8), calls=%async_computation | async-start | bytes 524288 | tf_op jit(solution)/shard_map/all_to_all | solution.py:302
  15.3 0.0 copy-start.3
  15.4 0.7 %copy-done.3 = s32[4096]{0:T(1024)S(1)} copy-done((s32[4096]{0:T(1024)S(1)}, s32[4096]{0:T(1024)}, u32[]{:S(2)}) %copy-start.3) | copy-done | bytes 16408
  16.1 0.0 copy-start.4
  16.1 0.7 %copy-done.4 = s32[32]{0:T(128)S(1)} copy-done((s32[32]{0:T(128)S(1)}, s32[32]{0:T(128)}, u32[]{:S(2)}) %copy-start.4) | copy-done | bytes 152
  16.7 0.3 plan.1.refs_0_
  17.0 0.0 copy-start
  17.0 0.0 copy-start.1
  17.0 0.0 copy-start.2
  17.0 1.7 %all-to-all-done.refs_1_ = bf16[64,16,128]{2,1,0:T(8,128)(2,1)S(1)} async-done(((bf16[64,16,128]{2,1,0:T(8,128)(2,1)}), bf16[64,16,128]{2,1,0:T(8,128)(2,1)S(1)}, u32[]{:S(2)}, u32[]{:S(2)}) %all-to-all-start) | async-done | bytes 262176 | tf_op jit(solution)/shard_map/all_to_all | solution.py:302
  18.7 6.7 %attend.1 = f32[64,5,4,128]{3,2,1,0:T(4,128)S(1)} custom-call(s32[1,128]{1,0:T(1,128)S(1)} %plan.1.refs_0_, bf16[64,16,128]{2,1,0:T(8,128)(2,1)S(1)} %all-to-all-done.refs_1_, bf16[64,4,128,128]{3,2,1,0:T(8,128)(2,1)} %refs_2_.2, bf16[64,4,128,128]{3,2,1,0:T(8,128)(2,1)} %refs_3_.2), custom_call_target="tpu_custom_call" | custom-call | tf_op jit(solution)/shard_map/attend/pallas_call | solution.py:189
  25.4 0.1 convert_element_type.4
  25.5 14.8 %all_to_all.10 = f16[64,5,4,128]{3,2,1,0:T(4,128)(2,1)S(1)} all-to-all(f16[64,5,4,128]{3,2,1,0:T(4,128)(2,1)S(1)} %convert_element_type.4), channel_id=1, replica_groups={{84,86,88,90,92,94,96,98,100,102,104,106,108,110,112,114,116,118,120,12..., dimensions={0} | all-to-all | bytes 655360 | tf_op jit(solution)/shard_map/all_to_all | solution.py:302
  40.3 0.1 convert_bitcast_fusion
  40.4 0.1 copy.8
  40.6 0.0 copy-done
  40.6 0.0 copy-done.1
  40.6 0.0 copy-done.2
  40.6 1.1 %merge.1 = bf16[4,4,128]{2,1,0:T(4,128)(2,1)} custom-call(f32[5,256,128]{2,1,0:T(8,128)S(1)} %bitcast.6, bf16[4,4,128]{2,1,0:T(4,128)(2,1)S(1)} %copy-done.2, bf16[32,4,128]{2,1,0:T(4,128)(2,1)S(1)} %copy-done, bf16[32,4,128]{2,1,0:T(4,128)(2,1)S(1)} %copy-done.1), custom_call_target="tpu_custom_call" | custom-call | tf_op jit(solution)/shard_map/merge/pallas_call | solution.py:325
Async XLA Ops:
  1.4 17.3 %all-to-all-start = ((bf16[64,16,128]{2,1,0:T(8,128)(2,1)}), bf16[64,16,128]{2,1,0:T(8,128)(2,1)S(1)}, u32[]{:S(2)}, u32[]{:S(2)}) async-start(bf16[64,16,128]{2,1,0:T(8,128)(2,1)} %broadcast_in_dim.8), calls=%async_computation | async-start | bytes 524288 | tf_op jit(solution)/shard_map/all_to_all | solution.py:302
  15.3 0.7 %copy-start.3 = (s32[4096]{0:T(1024)S(1)}, s32[4096]{0:T(1024)}, u32[]{:S(2)}) copy-start(s32[4096]{0:T(1024)} %param.13) | copy-start | bytes 49156
  16.1 0.7 %copy-start.4 = (s32[32]{0:T(128)S(1)}, s32[32]{0:T(128)}, u32[]{:S(2)}) copy-start(s32[32]{0:T(128)} %param.12) | copy-start | bytes 388
  17.0 23.6 %copy-start = (bf16[32,4,128]{2,1,0:T(4,128)(2,1)S(1)}, bf16[32,4,128]{2,1,0:T(4,128)(2,1)}, u32[]{:S(2)}) copy-start(bf16[32,4,128]{2,1,0:T(4,128)(2,1)} %refs_2_.3) | copy-start | bytes 98308
  17.0 23.6 %copy-start.1 = (bf16[32,4,128]{2,1,0:T(4,128)(2,1)S(1)}, bf16[32,4,128]{2,1,0:T(4,128)(2,1)}, u32[]{:S(2)}) copy-start(bf16[32,4,128]{2,1,0:T(4,128)(2,1)} %refs_3_.3) | copy-start | bytes 98308
  17.0 23.6 %copy-start.2 = (bf16[4,4,128]{2,1,0:T(4,128)(2,1)S(1)}, bf16[4,4,128]{2,1,0:T(4,128)(2,1)}, u32[]{:S(2)}) copy-start(bf16[4,4,128]{2,1,0:T(4,128)(2,1)} %refs_1_.1) | copy-start | bytes 12292

commit v4 on v3

--- a/solution.py
+++ b/solution.py
@@ -12,8 +12,7 @@
 NO_SCORE = -480000.0
 MOST_POWER = 120.0
 GROUP = 8
-QUERY_FIRST = 42
-RESULT_FIRST = 42
+FIRST = 42
 MIB = 1024 * 1024
 
 
@@ -23,6 +22,9 @@
 ):
     pages = k_ref.shape[0]
     seqs, pairs = q_ref.shape[0], q_ref.shape[1]
+    page_bits, group_bits = pages.bit_length() - 1, GROUP.bit_length() - 1
+    code_bits = page_bits + seqs.bit_length() - 1
+    shift = lax.shift_right_logical
     token = lax.broadcasted_iota(jnp.int32, (8, 128), 1)
     upper = lax.broadcasted_iota(jnp.int32, (8, 128), 0) < 4
 
@@ -30,15 +32,15 @@
         return list_ref[i] & (pages - 1)
 
     def seq_of(i):
-        return (list_ref[i] // pages) & (seqs - 1)
+        return shift(list_ref[i], page_bits) & (seqs - 1)
 
     def start(hbm, vmem, sem, i):
-        pltpu.make_async_copy(hbm.at[page_of(i)], vmem.at[i], sem.at[i // GROUP]).start()
+        pltpu.make_async_copy(hbm.at[page_of(i)], vmem.at[i], sem.at[shift(i, group_bits)]).start()
 
     def find(p, count):
         code = plan_ref[0, p]
         used = code >= seqs
-        list_ref[count] = code * pages + p
+        list_ref[count] = (code << page_bits) + p
 
         @pl.when(used)
         def _():
@@ -47,7 +49,7 @@
         return count + used.astype(jnp.int32)
 
     count = lax.fori_loop(0, pages, find, 0, unroll=4)
-    groups = jnp.maximum((count + GROUP - 1) // GROUP, 1)
+    groups = jnp.maximum(shift(count + GROUP - 1, group_bits), 1)
 
     def pad(i, _):
         list_ref[i] = 0
@@ -70,10 +72,11 @@
     def regroup(s, _):
         for h in range(2):
             for j in range(pairs):
-                q_ref[s, j, 8 * h : 8 * h + 8] = arrived_ref[(2 * s + h - QUERY_FIRST) % (2 * seqs), 8 * j : 8 * j + 8]
+                q_ref[s, j, 8 * h : 8 * h + 8] = arrived_ref[(2 * s + h - FIRST) % (2 * seqs), 8 * j : 8 * j + 8]
         return 0
 
-    lax.fori_loop(0, seqs, regroup, 0, unroll=4)
+    for s in range(seqs):
+        regroup(s, 0)
 
     def each(g, body):
         for u in range(GROUP):
@@ -96,7 +99,7 @@
 
     def weigh(i):
         s = seq_of(i)
-        inside = token < list_ref[i] // (pages * seqs)
+        inside = token < shift(list_ref[i], code_bits)
         for j in range(pairs):
             for h in range(2):
                 score = jnp.where(inside, score_ref[i, j, h], LOWEST)
@@ -142,37 +145,51 @@
     kind = token & 3
     first = (token & 4) == 0
     block = lax.shift_right_logical(token, 3)
+    is_score = kind < pairs
 
     def rounded(x):
         return x.astype(jnp.bfloat16).astype(jnp.float32)
 
+    def halves(one, two):
+        low = jnp.where(upper, one, pltpu.roll(two, 4, 0))
+        high = jnp.where(upper, pltpu.roll(one, 4, 0), two)
+        return jnp.where(first, low, high)
+
     def pack(s, _):
+        places = [(2 * s + h - FIRST) % (2 * seqs) for h in range(2)]
+        outs = [[out_ref[s, j, h] for j in range(pairs)] for h in range(2)]
+        largest = jnp.abs(outs[0][0])
+        for out in outs[0][1:] + outs[1]:
+            largest = jnp.maximum(largest, jnp.abs(out))
+        largest = jnp.max(largest, axis=1, keepdims=True)
+        power = jnp.clip(jnp.ceil(-jnp.log2(largest)), 0.0, MOST_POWER)
+        power = jnp.broadcast_to(power, (8, 128))
+        factor = jnp.exp2(power)
+        notes = []
         for h in range(2):
-            to = (2 * s + h - RESULT_FIRST) & (2 * seqs - 1)
-            note = jnp.zeros((8, 128), jnp.float32)
-            powers = jnp.zeros((8, 128), jnp.float32)
+            note = max_ref[s, 0, h]
+            for j in range(1, pairs):
+                note = jnp.where(kind == j, max_ref[s, j, h], note)
             for j in range(pairs):
-                out = out_ref[s, j, h]
-                largest = jnp.max(jnp.abs(out), axis=1, keepdims=True)
-                power = jnp.clip(jnp.ceil(-jnp.log2(largest)), 0.0, MOST_POWER)
-                out = out * jnp.exp2(power)
-                send_ref[to, 2 * j] = out[:4]
-                send_ref[to, 2 * j + 1] = out[4:]
+                out = outs[h][j] * factor
+                send_ref[places[h], 2 * j] = out[:4]
+                send_ref[places[h], 2 * j + 1] = out[4:]
                 total = jnp.sum(sum_ref[s, j, h], axis=1, keepdims=True)
-                best = jnp.maximum(max_ref[s, j, h], NO_SCORE) * SCORE_UNIT
-                note = jnp.where(kind == j, best, note)
                 note = jnp.where(kind == pairs + j, total, note)
-                powers = jnp.where(kind == j, power, powers)
-            note = jnp.where(first, note, pltpu.roll(note, 4, 0))
-            powers = jnp.where(first, powers, pltpu.roll(powers, 4, 0))
-            high = rounded(note)
-            middle = rounded(note - high)
-            low = note - high - middle
-            note = jnp.where(block == 0, high, jnp.where(block == 1, middle, low))
-            send_ref[to, 2 * pairs] = jnp.where(block < 3, note, powers)[:4]
+            notes.append(note)
+        note = halves(*notes)
+        note = jnp.where(is_score, jnp.maximum(note, NO_SCORE) * SCORE_UNIT, note)
+        high = rounded(note)
+        rest = note - high
+        middle = rounded(rest)
+        note = jnp.where(block == 0, high, jnp.where(block == 1, middle, rest - middle))
+        note = jnp.where(block < 3, note, halves(power, power))
+        send_ref[places[0], 2 * pairs] = note[:4]
+        send_ref[places[1], 2 * pairs] = note[4:]
         return 0
 
-    lax.fori_loop(0, seqs, pack, 0, unroll=4)
+    for s in range(seqs):
+        pack(s, 0)
 
 
 def attend(plan, arrived, key_cache, value_cache):
@@ -296,9 +313,9 @@
     )(page_table.reshape(seqs, slots), lengths.reshape(1, seqs))
 
 
-def exchange(x, first):
+def exchange(x):
     devices = x.shape[0]
-    order = [(d + first) % devices for d in range(devices)]
+    order = [(d + FIRST) % devices for d in range(devices)]
     return lax.all_to_all(x, "kv", 0, 0, tiled=True, axis_index_groups=[order])
 
 
@@ -314,12 +331,12 @@
     kv_index = lax.axis_index("kv")
 
     mine = queries.reshape(rows, head_width)
-    arrived = exchange(jnp.broadcast_to(mine[None], (devices, rows, head_width)), QUERY_FIRST)
+    arrived = exchange(jnp.broadcast_to(mine[None], (devices, rows, head_width)))
     plan = plan_pages(pages_here, page_len, lengths, page_table)
     sent = attend(plan, arrived, key_cache, value_cache)
 
     vmem = pl.BlockSpec(memory_space=pltpu.VMEM)
-    received = exchange(sent.astype(jnp.float16), RESULT_FIRST).astype(jnp.float32)
+    received = exchange(sent.astype(jnp.float16)).astype(jnp.float32)
     received = jnp.transpose(received, (1, 0, 2, 3)).reshape(kv_here + 1, devices * local_rows, head_width)
 
     return pl.pallas_call(

time: 41.9 us -> 41.7 us (level)
  Pallas kernels: 8.02 us -> 6.5 us
  blocking collectives: 14.8 us -> 15.9 us
    pallas_call x1, Pallas kernels: 6.68 us -> 5.16 us  [attend(): pl.pallas_call(lambda *refs: attend_kernel(scale2, *refs), out_shape=jax....]
    all_to_all x1, blocking collectives: 14.8 us -> 15.9 us  [exchange(): return lax.all_to_all(x, 'kv', 0, 0, tiled=True, axis_index_groups=[order])]
where the time goes in v4:
time: 41.7 us; the launch traced here: 41.2 us
  blocking collectives  15.9 us (38%)
  starting transfers between devices  13.9 us (33%)
  Pallas kernels  6.5 us (16%)
  local copies, waits for them, and re-layouts  2.92 us (7%)
  waiting for transfers between devices  1.68 us (4%)
    all_to_all x1, blocking collectives, exchange(): return lax.all_to_all(x, 'kv', 0, 0, tiled=True, axis_index_groups=[order])  15.9 us
    all_to_all x1, starting transfers between devices, exchange(): return lax.all_to_all(x, 'kv', 0, 0, tiled=True, axis_index_groups=[order])  13.9 us
    pallas_call x1, Pallas kernels, attend(): pl.pallas_call(lambda *refs: attend_kernel(scale2, *refs), out_shape=jax....  5.16 us
    all_to_all x1, waiting for transfers between devices, exchange(): return lax.all_to_all(x, 'kv', 0, 0, tiled=True, axis_index_groups=[order])  1.68 us
    broadcast_in_dim x1, local copies, waits for them, and re-layouts, on_device(): jnp.broadcast_to(mine[None], (devices, rows, head_width))  1.42 us
    unnamed x10, local copies, waits for them, and re-layouts  1.39 us
    pallas_call x1, Pallas kernels, on_device(): pl.pallas_call(lambda *refs: merge_kernel(scale2, *refs), out_shape=jax.S...  1.08 us
  transfers between devices with their start and end apart: 1, of which 1 were waited for; matrix products, arithmetic and copies ran while one was open for 0% of the time, Pallas kernels for 1%

profile of v4, /device:TPU:0, one launch (start us, length us, event | category | flops | bytes accessed | tf_op | source)
XLA Modules:
  0.0 41.2 jit_solution(10994368775663390315)
XLA Ops:
  0.0 1.4 %broadcast_in_dim.8 = bf16[64,16,128]{2,1,0:T(8,128)(2,1)} broadcast(bf16[16,128]{1,0:T(8,128)(2,1)} %bitcast.7), dimensions={1,2} | broadcast | bytes 266240 | tf_op jit(solution)/shard_map/broadcast_in_dim | solution.py:334
  1.4 13.9 %all-to-all-start = ((bf16[64,16,128]{2,1,0:T(8,128)(2,1)}), bf16[64,16,128]{2,1,0:T(8,128)(2,1)S(1)}, u32[]{:S(2)}, u32[]{:S(2)}) async-start(bf16[64,16,128]{2,1,0:T(8,128)(2,1)} %broadcast_in_dim.8), calls=%async_computation | async-start | bytes 524288 | tf_op jit(solution)/shard_map/all_to_all | solution.py:319
  15.3 0.0 copy-start.3
  15.4 0.7 %copy-done.3 = s32[4096]{0:T(1024)S(1)} copy-done((s32[4096]{0:T(1024)S(1)}, s32[4096]{0:T(1024)}, u32[]{:S(2)}) %copy-start.3) | copy-done | bytes 16408
  16.1 0.0 copy-start.4
  16.1 0.7 %copy-done.4 = s32[32]{0:T(128)S(1)} copy-done((s32[32]{0:T(128)S(1)}, s32[32]{0:T(128)}, u32[]{:S(2)}) %copy-start.4) | copy-done | bytes 152
  16.7 0.3 plan.1.refs_0_
  17.0 0.0 copy-start
  17.0 0.0 copy-start.1
  17.0 0.0 copy-start.2
  17.0 1.7 %all-to-all-done.refs_1_ = bf16[64,16,128]{2,1,0:T(8,128)(2,1)S(1)} async-done(((bf16[64,16,128]{2,1,0:T(8,128)(2,1)}), bf16[64,16,128]{2,1,0:T(8,128)(2,1)S(1)}, u32[]{:S(2)}, u32[]{:S(2)}) %all-to-all-start) | async-done | bytes 262176 | tf_op jit(solution)/shard_map/all_to_all | solution.py:319
  18.7 5.2 %attend.1 = f32[64,5,4,128]{3,2,1,0:T(4,128)S(1)} custom-call(s32[1,128]{1,0:T(1,128)S(1)} %plan.1.refs_0_, bf16[64,16,128]{2,1,0:T(8,128)(2,1)S(1)} %all-to-all-done.refs_1_, bf16[64,4,128,128]{3,2,1,0:T(8,128)(2,1)} %refs_2_.2, bf16[64,4,128,128]{3,2,1,0:T(8,128)(2,1)} %refs_3_.2), custom_call_target="tpu_custom_call" | custom-call | tf_op jit(solution)/shard_map/attend/pallas_call | solution.py:206
  23.9 0.1 convert_element_type.4
  24.0 15.9 %all_to_all.10 = f16[64,5,4,128]{3,2,1,0:T(4,128)(2,1)S(1)} all-to-all(f16[64,5,4,128]{3,2,1,0:T(4,128)(2,1)S(1)} %convert_element_type.4), channel_id=1, replica_groups={{84,86,88,90,92,94,96,98,100,102,104,106,108,110,112,114,116,118,120,12..., dimensions={0} | all-to-all | bytes 655360 | tf_op jit(solution)/shard_map/all_to_all | solution.py:319
  39.9 0.1 convert_bitcast_fusion
  40.0 0.1 copy.8
  40.1 0.0 copy-done
  40.1 0.0 copy-done.1
  40.1 0.0 copy-done.2
  40.2 1.1 %merge.1 = bf16[4,4,128]{2,1,0:T(4,128)(2,1)} custom-call(f32[5,256,128]{2,1,0:T(8,128)S(1)} %bitcast.6, bf16[4,4,128]{2,1,0:T(4,128)(2,1)S(1)} %copy-done.2, bf16[32,4,128]{2,1,0:T(4,128)(2,1)S(1)} %copy-done, bf16[32,4,128]{2,1,0:T(4,128)(2,1)S(1)} %copy-done.1), custom_call_target="tpu_custom_call" | custom-call | tf_op jit(solution)/shard_map/merge/pallas_call | solution.py:342
Async XLA Ops:
  1.4 17.3 %all-to-all-start = ((bf16[64,16,128]{2,1,0:T(8,128)(2,1)}), bf16[64,16,128]{2,1,0:T(8,128)(2,1)S(1)}, u32[]{:S(2)}, u32[]{:S(2)}) async-start(bf16[64,16,128]{2,1,0:T(8,128)(2,1)} %broadcast_in_dim.8), calls=%async_computation | async-start | bytes 524288 | tf_op jit(solution)/shard_map/all_to_all | solution.py:319
  15.3 0.7 %copy-start.3 = (s32[4096]{0:T(1024)S(1)}, s32[4096]{0:T(1024)}, u32[]{:S(2)}) copy-start(s32[4096]{0:T(1024)} %param.13) | copy-start | bytes 49156
  16.1 0.7 %copy-start.4 = (s32[32]{0:T(128)S(1)}, s32[32]{0:T(128)}, u32[]{:S(2)}) copy-start(s32[32]{0:T(128)} %param.12) | copy-start | bytes 388
  17.0 23.1 %copy-start = (bf16[32,4,128]{2,1,0:T(4,128)(2,1)S(1)}, bf16[32,4,128]{2,1,0:T(4,128)(2,1)}, u32[]{:S(2)}) copy-start(bf16[32,4,128]{2,1,0:T(4,128)(2,1)} %refs_2_.3) | copy-start | bytes 98308
  17.0 23.1 %copy-start.1 = (bf16[32,4,128]{2,1,0:T(4,128)(2,1)S(1)}, bf16[32,4,128]{2,1,0:T(4,128)(2,1)}, u32[]{:S(2)}) copy-start(bf16[32,4,128]{2,1,0:T(4,128)(2,1)} %refs_3_.3) | copy-start | bytes 98308
  17.0 23.1 %copy-start.2 = (bf16[4,4,128]{2,1,0:T(4,128)(2,1)S(1)}, bf16[4,4,128]{2,1,0:T(4,128)(2,1)}, u32[]{:S(2)}) copy-start(bf16[4,4,128]{2,1,0:T(4,128)(2,1)} %refs_1_.1) | copy-start | bytes 12292

commit v5 on v4

--- a/solution.py
+++ b/solution.py
@@ -34,8 +34,8 @@
     def seq_of(i):
         return shift(list_ref[i], page_bits) & (seqs - 1)
 
-    def start(hbm, vmem, sem, i):
-        pltpu.make_async_copy(hbm.at[page_of(i)], vmem.at[i], sem.at[shift(i, group_bits)]).start()
+    def start(hbm, vmem, sem, i, priority=0):
+        pltpu.make_async_copy(hbm.at[page_of(i)], vmem.at[i], sem.at[shift(i, group_bits)]).start(priority=priority)
 
     def find(p, count):
         code = plan_ref[0, p]
@@ -60,7 +60,7 @@
 
     def rest(g, _):
         for u in range(GROUP):
-            start(v_hbm, v_ref, v_sem, g * GROUP + u)
+            start(v_hbm, v_ref, v_sem, g * GROUP + u, priority=1)
         return 0
 
     lax.fori_loop(0, groups, rest, 0)

time: 41.7 us -> 41.6 us (level)
  no operation moved by 1% of the time
where the time goes in v5:
time: 41.6 us; the launch traced here: 41.2 us
  blocking collectives  15.8 us (38%)
  starting transfers between devices  13.9 us (33%)
  Pallas kernels  6.59 us (16%)
  local copies, waits for them, and re-layouts  2.92 us (7%)
  waiting for transfers between devices  1.68 us (4%)
    all_to_all x1, blocking collectives, exchange(): return lax.all_to_all(x, 'kv', 0, 0, tiled=True, axis_index_groups=[order])  15.8 us
    all_to_all x1, starting transfers between devices, exchange(): return lax.all_to_all(x, 'kv', 0, 0, tiled=True, axis_index_groups=[order])  13.9 us
    pallas_call x1, Pallas kernels, attend(): pl.pallas_call(lambda *refs: attend_kernel(scale2, *refs), out_shape=jax....  5.25 us
    all_to_all x1, waiting for transfers between devices, exchange(): return lax.all_to_all(x, 'kv', 0, 0, tiled=True, axis_index_groups=[order])  1.68 us
    broadcast_in_dim x1, local copies, waits for them, and re-layouts, on_device(): jnp.broadcast_to(mine[None], (devices, rows, head_width))  1.42 us
    unnamed x10, local copies, waits for them, and re-layouts  1.39 us
    pallas_call x1, Pallas kernels, on_device(): pl.pallas_call(lambda *refs: merge_kernel(scale2, *refs), out_shape=jax.S...  1.08 us
  transfers between devices with their start and end apart: 1, of which 1 were waited for; matrix products, arithmetic and copies ran while one was open for 0% of the time, Pallas kernels for 1%

profile of v5, /device:TPU:0, one launch (start us, length us, event | category | flops | bytes accessed | tf_op | source)
XLA Modules:
  0.0 41.2 jit_solution(11852272978063549)
XLA Ops:
  0.0 1.4 %broadcast_in_dim.8 = bf16[64,16,128]{2,1,0:T(8,128)(2,1)} broadcast(bf16[16,128]{1,0:T(8,128)(2,1)} %bitcast.7), dimensions={1,2} | broadcast | bytes 266240 | tf_op jit(solution)/shard_map/broadcast_in_dim | solution.py:334
  1.4 13.9 %all-to-all-start = ((bf16[64,16,128]{2,1,0:T(8,128)(2,1)}), bf16[64,16,128]{2,1,0:T(8,128)(2,1)S(1)}, u32[]{:S(2)}, u32[]{:S(2)}) async-start(bf16[64,16,128]{2,1,0:T(8,128)(2,1)} %broadcast_in_dim.8), calls=%async_computation | async-start | bytes 524288 | tf_op jit(solution)/shard_map/all_to_all | solution.py:319
  15.3 0.0 copy-start.3
  15.4 0.7 %copy-done.3 = s32[4096]{0:T(1024)S(1)} copy-done((s32[4096]{0:T(1024)S(1)}, s32[4096]{0:T(1024)}, u32[]{:S(2)}) %copy-start.3) | copy-done | bytes 16408
  16.1 0.0 copy-start.4
  16.1 0.7 %copy-done.4 = s32[32]{0:T(128)S(1)} copy-done((s32[32]{0:T(128)S(1)}, s32[32]{0:T(128)}, u32[]{:S(2)}) %copy-start.4) | copy-done | bytes 152
  16.7 0.3 plan.1.refs_0_
  17.0 0.0 copy-start
  17.0 0.0 copy-start.1
  17.0 0.0 copy-start.2
  17.0 1.7 %all-to-all-done.refs_1_ = bf16[64,16,128]{2,1,0:T(8,128)(2,1)S(1)} async-done(((bf16[64,16,128]{2,1,0:T(8,128)(2,1)}), bf16[64,16,128]{2,1,0:T(8,128)(2,1)S(1)}, u32[]{:S(2)}, u32[]{:S(2)}) %all-to-all-start) | async-done | bytes 262176 | tf_op jit(solution)/shard_map/all_to_all | solution.py:319
  18.7 5.2 %attend.1 = f32[64,5,4,128]{3,2,1,0:T(4,128)S(1)} custom-call(s32[1,128]{1,0:T(1,128)S(1)} %plan.1.refs_0_, bf16[64,16,128]{2,1,0:T(8,128)(2,1)S(1)} %all-to-all-done.refs_1_, bf16[64,4,128,128]{3,2,1,0:T(8,128)(2,1)} %refs_2_.2, bf16[64,4,128,128]{3,2,1,0:T(8,128)(2,1)} %refs_3_.2), custom_call_target="tpu_custom_call" | custom-call | tf_op jit(solution)/shard_map/attend/pallas_call | solution.py:206
  24.0 0.1 convert_element_type.4
  24.1 15.8 %all_to_all.10 = f16[64,5,4,128]{3,2,1,0:T(4,128)(2,1)S(1)} all-to-all(f16[64,5,4,128]{3,2,1,0:T(4,128)(2,1)S(1)} %convert_element_type.4), channel_id=1, replica_groups={{84,86,88,90,92,94,96,98,100,102,104,106,108,110,112,114,116,118,120,12..., dimensions={0} | all-to-all | bytes 655360 | tf_op jit(solution)/shard_map/all_to_all | solution.py:319
  39.8 0.1 convert_bitcast_fusion
  40.0 0.1 copy.8
  40.1 0.0 copy-done
  40.1 0.0 copy-done.1
  40.1 0.0 copy-done.2
  40.1 1.1 %merge.1 = bf16[4,4,128]{2,1,0:T(4,128)(2,1)} custom-call(f32[5,256,128]{2,1,0:T(8,128)S(1)} %bitcast.6, bf16[4,4,128]{2,1,0:T(4,128)(2,1)S(1)} %copy-done.2, bf16[32,4,128]{2,1,0:T(4,128)(2,1)S(1)} %copy-done, bf16[32,4,128]{2,1,0:T(4,128)(2,1)S(1)} %copy-done.1), custom_call_target="tpu_custom_call" | custom-call | tf_op jit(solution)/shard_map/merge/pallas_call | solution.py:342
Async XLA Ops:
  1.4 17.3 %all-to-all-start = ((bf16[64,16,128]{2,1,0:T(8,128)(2,1)}), bf16[64,16,128]{2,1,0:T(8,128)(2,1)S(1)}, u32[]{:S(2)}, u32[]{:S(2)}) async-start(bf16[64,16,128]{2,1,0:T(8,128)(2,1)} %broadcast_in_dim.8), calls=%async_computation | async-start | bytes 524288 | tf_op jit(solution)/shard_map/all_to_all | solution.py:319
  15.3 0.7 %copy-start.3 = (s32[4096]{0:T(1024)S(1)}, s32[4096]{0:T(1024)}, u32[]{:S(2)}) copy-start(s32[4096]{0:T(1024)} %param.13) | copy-start | bytes 49156
  16.1 0.7 %copy-start.4 = (s32[32]{0:T(128)S(1)}, s32[32]{0:T(128)}, u32[]{:S(2)}) copy-start(s32[32]{0:T(128)} %param.12) | copy-start | bytes 388
  17.0 23.1 %copy-start = (bf16[32,4,128]{2,1,0:T(4,128)(2,1)S(1)}, bf16[32,4,128]{2,1,0:T(4,128)(2,1)}, u32[]{:S(2)}) copy-start(bf16[32,4,128]{2,1,0:T(4,128)(2,1)} %refs_2_.3) | copy-start | bytes 98308
  17.0 23.1 %copy-start.1 = (bf16[32,4,128]{2,1,0:T(4,128)(2,1)S(1)}, bf16[32,4,128]{2,1,0:T(4,128)(2,1)}, u32[]{:S(2)}) copy-start(bf16[32,4,128]{2,1,0:T(4,128)(2,1)} %refs_3_.3) | copy-start | bytes 98308
  17.0 23.1 %copy-start.2 = (bf16[4,4,128]{2,1,0:T(4,128)(2,1)S(1)}, bf16[4,4,128]{2,1,0:T(4,128)(2,1)}, u32[]{:S(2)}) copy-start(bf16[4,4,128]{2,1,0:T(4,128)(2,1)} %refs_1_.1) | copy-start | bytes 12292
